TPU v7x, 32 devices: a whole 2x2x4 slice. The times are simulated.
32 devices in a mesh: pipe: 2 (over y), dp: 16 (over z, x, core).
Axes of the slice: x: 2, y: 2, z: 4, core: 2. Of those that a mesh axis runs over, the one named last changes fastest.
Arguments:
- tokens: bfloat16 [6144, 1536], P('dp'), may hold values from -6 to 6
- cotangent: bfloat16 [6144, 1536], P('dp'), may hold values from -6 to 6
- seq_lengths: int32 [48, 8], P('dp'), may hold values from 0 to 128, as said below
- w_query: bfloat16 [2, 1536, 1536], P('pipe', 'dp'), may hold values from -0.15625 to 0.15625
- w_key: bfloat16 [2, 1536, 768], P('pipe', 'dp'), may hold values from -0.15625 to 0.15625
- w_value: bfloat16 [2, 1536, 768], P('pipe', 'dp'), may hold values from -0.15625 to 0.15625
- w_out: bfloat16 [2, 1536, 1536], P('pipe', 'dp'), may hold values from -1.25 to 1.25
- w_gate: bfloat16 [2, 1536, 4096], P('pipe', 'dp'), may hold values from -0.15625 to 0.15625
- w_up: bfloat16 [2, 1536, 4096], P('pipe', 'dp'), may hold values from -0.15625 to 0.15625
- w_down: bfloat16 [2, 4096, 1536], P('pipe', 'dp'), may hold values from -0.09375 to 0.09375
- gain_attn: bfloat16 [2, 1536], P('pipe', 'dp'), may hold values from 0.25 to 1.75
- gain_ffn: bfloat16 [2, 1536], P('pipe', 'dp'), may hold values from 0.25 to 1.75
Outputs:
- layer_outputs: bfloat16 [2, 6144, 1536], P('pipe', 'dp')
- input_grads: bfloat16 [2, 6144, 1536], P('pipe', 'dp')
- grad_query: float32 [2, 1536, 1536], P('pipe', 'dp')
- grad_key: float32 [2, 1536, 768], P('pipe', 'dp')
- grad_value: float32 [2, 1536, 768], P('pipe', 'dp')
- grad_out: float32 [2, 1536, 1536], P('pipe', 'dp')
- grad_gate: float32 [2, 1536, 4096], P('pipe', 'dp')
- grad_up: float32 [2, 1536, 4096], P('pipe', 'dp')
- grad_down: float32 [2, 4096, 1536], P('pipe', 'dp')
- grad_gain_attn: float32 [2, 1536], P('pipe', 'dp')
- grad_gain_ffn: float32 [2, 1536], P('pipe', 'dp')
Inputs may be any that keep to these rules, and one draw needn't show every extreme that they name: `seq_lengths`: each row lists the lengths of the sequences packed in order into one micro-batch row of 128 slots; zeros stand for unused entries, a row's lengths sum to at most 128, and the slots after its last sequence form one more sequence.
All inputs are finite; a program needn't handle non-finite values.
Results may differ from a plain program's by a relative error of at most 0.023.
Values may be sent and summed in bfloat16 or wider, within the bound.
A program may use at most 256 MiB of HBM per device.

v0:
```python
import math

import jax
import jax.numpy as jnp
from jax import lax
from jax.sharding import PartitionSpec as P

HEADS = 16
KV_HEADS = 8
HD = 96
FF = 4096


EPSILON = 1e-05
ROPE_BASE = 100000.0


def passed_along(array, axis, by):
    count = lax.axis_size(axis)
    pairs = [(i, i + by) for i in range(count) if 0 <= i + by < count]
    return lax.ppermute(array, axis, pairs)


def row_starts(lengths, row_length):
    seq_ends = jnp.cumsum(lengths, axis=-1)
    slot_ids = jnp.arange(row_length, dtype=jnp.int32)
    reached = jnp.where(seq_ends[:, None, :] <= slot_ids[None, :, None], seq_ends[:, None, :], 0)
    return jnp.max(reached, axis=-1)


def rotary_tables(seg_start):
    row_length = seg_start.shape[0]
    half_dim = HD // 2
    places = (jnp.arange(row_length, dtype=jnp.int32) - seg_start).astype(jnp.float32)
    inv_freqs = jnp.exp(jnp.arange(half_dim, dtype=jnp.float32) * (-2.0 * math.log(ROPE_BASE) / HD))
    angles = places[:, None] * inv_freqs[None, :]
    return (jnp.cos(angles)[:, None, :], jnp.sin(angles)[:, None, :])


def rotate(operand, cosine, sine_part):
    half_dim = operand.shape[-1] // 2
    front_half, back_half = (operand[..., :half_dim], operand[..., half_dim:])
    return jnp.concatenate(
        [front_half * cosine - back_half * sine_part, back_half * cosine + front_half * sine_part],
        axis=-1,
    )


def rotate_back(incoming, cosine, sine_part):
    half_dim = incoming.shape[-1] // 2
    front_half, back_half = (incoming[..., :half_dim], incoming[..., half_dim:])
    return jnp.concatenate(
        [front_half * cosine + back_half * sine_part, back_half * cosine - front_half * sine_part],
        axis=-1,
    )


def attend_mask(seg_start):
    row_length = seg_start.shape[0]
    slot_ids = jnp.arange(row_length, dtype=jnp.int32)
    return (seg_start[None, :] == seg_start[:, None]) & (slot_ids[None, :] <= slot_ids[:, None])


def inv_rms(operand):
    return lax.rsqrt(jnp.mean(operand * operand, axis=-1, keepdims=True) + EPSILON)


def times_transposed(first_operand, second_operand):
    return lax.dot_general(
        first_operand, second_operand, (((1,), (1,)), ((), ())), preferred_element_type=jnp.float32
    )


def across_rows(first_operand, second_operand):
    return lax.dot_general(
        first_operand, second_operand, (((0,), (0,)), ((), ())), preferred_element_type=jnp.float32
    )


def scores_of(query_rot, key_rot, seg_start):
    row_length = query_rot.shape[0]
    grouped = query_rot.reshape(row_length, KV_HEADS, HEADS // KV_HEADS, HD)
    raw_scores = jnp.einsum(
        "tkgd,skd->kgts", grouped, key_rot, preferred_element_type=jnp.float32
    ) * (1.0 / math.sqrt(HD))
    return (jnp.where(attend_mask(seg_start), raw_scores, -1e30), grouped)


def forward_unit(params, input_low, seg_start):
    w_query, w_key, w_value, w_out, w_gate, w_up, w_down, gain_one, gain_two = params
    row_length = input_low.shape[0]
    hidden = input_low.astype(jnp.float32)
    normed = hidden * inv_rms(hidden)
    attn_input = (normed * gain_one.astype(jnp.float32)).astype(jnp.bfloat16)
    cosine, sine_part = rotary_tables(seg_start)
    query_proj = jnp.dot(attn_input, w_query, preferred_element_type=jnp.float32).reshape(
        row_length, HEADS, HD
    )
    key_proj = jnp.dot(attn_input, w_key, preferred_element_type=jnp.float32).reshape(
        row_length, KV_HEADS, HD
    )
    value_proj = jnp.dot(attn_input, w_value, preferred_element_type=jnp.float32).reshape(
        row_length, KV_HEADS, HD
    )
    query_rot = rotate(query_proj, cosine, sine_part).astype(jnp.bfloat16)
    key_rot = rotate(key_proj, cosine, sine_part).astype(jnp.bfloat16)
    value_low = value_proj.astype(jnp.bfloat16)
    scores, grouped = scores_of(query_rot, key_rot, seg_start)
    row_max = jnp.max(scores, axis=-1, keepdims=True)
    exp_scores = jnp.exp(scores - row_max)
    exp_total = jnp.sum(exp_scores, axis=-1, keepdims=True)
    log_total = row_max + jnp.log(exp_total)
    probs_low = (exp_scores / exp_total).astype(jnp.bfloat16)
    attended = jnp.einsum(
        "kgts,skd->tkgd", probs_low, value_low, preferred_element_type=jnp.float32
    )
    attended = attended.reshape(row_length, HEADS * HD).astype(jnp.bfloat16)
    mid_stream = hidden + jnp.dot(attended, w_out, preferred_element_type=jnp.float32)
    normed_two = mid_stream * inv_rms(mid_stream)
    ffn_input = (normed_two * gain_two.astype(jnp.float32)).astype(jnp.bfloat16)
    gate_proj = jnp.dot(ffn_input, w_gate, preferred_element_type=jnp.float32)
    up_proj = jnp.dot(ffn_input, w_up, preferred_element_type=jnp.float32)
    activated = (jax.nn.silu(gate_proj) * up_proj).astype(jnp.bfloat16)
    result = mid_stream + jnp.dot(activated, w_down, preferred_element_type=jnp.float32)
    kept_values = (
        input_low,
        attn_input,
        query_rot,
        key_rot,
        value_low,
        log_total,
        attended,
        mid_stream,
        ffn_input,
        gate_proj,
        up_proj,
        activated,
    )
    return (result.astype(jnp.bfloat16), kept_values)


def backward_unit(params, kept_values, seg_start, incoming):
    w_query, w_key, w_value, w_out, w_gate, w_up, w_down, gain_one, gain_two = params
    (
        input_low,
        attn_input,
        query_rot,
        key_rot,
        value_low,
        log_total,
        attended,
        mid_stream,
        ffn_input,
        gate_proj,
        up_proj,
        activated,
    ) = kept_values
    row_length = input_low.shape[0]
    group_size = HEADS // KV_HEADS
    scale_factor = 1.0 / math.sqrt(HD)
    hidden = input_low.astype(jnp.float32)
    first_inv = inv_rms(hidden)
    normed = hidden * first_inv
    second_inv = inv_rms(mid_stream)
    normed_two = mid_stream * second_inv
    down_grad = incoming.astype(jnp.bfloat16)
    act_grad = times_transposed(down_grad, w_down)
    sigmoid_gate = jax.nn.sigmoid(gate_proj)
    gate_grad = (
        act_grad * up_proj * sigmoid_gate * (1.0 + gate_proj * (1.0 - sigmoid_gate))
    ).astype(jnp.bfloat16)
    up_grad = (act_grad * gate_proj * sigmoid_gate).astype(jnp.bfloat16)
    ffn_grad = times_transposed(gate_grad, w_gate) + times_transposed(up_grad, w_up)
    gain_two_grad = jnp.sum(ffn_grad * normed_two, axis=0)
    scaled_two = ffn_grad * gain_two.astype(jnp.float32)
    mid_grad = incoming + second_inv * (
        scaled_two - normed_two * jnp.mean(scaled_two * normed_two, axis=-1, keepdims=True)
    )
    out_grad = mid_grad.astype(jnp.bfloat16)
    attended_grad = (
        times_transposed(out_grad, w_out)
        .astype(jnp.bfloat16)
        .reshape(row_length, KV_HEADS, group_size, HD)
    )
    scores, grouped = scores_of(query_rot, key_rot, seg_start)
    attn_probs = jnp.exp(scores - log_total)
    probs_low = attn_probs.astype(jnp.bfloat16)
    prob_grad = jnp.einsum(
        "tkgd,skd->kgts", attended_grad, value_low, preferred_element_type=jnp.float32
    )
    value_grad = jnp.einsum(
        "kgts,tkgd->skd", probs_low, attended_grad, preferred_element_type=jnp.float32
    )
    value_grad = value_grad.reshape(row_length, KV_HEADS * HD).astype(jnp.bfloat16)
    score_grad = (
        attn_probs * (prob_grad - jnp.sum(attn_probs * prob_grad, axis=-1, keepdims=True))
    ).astype(jnp.bfloat16)
    rot_query_grad = (
        jnp.einsum(
            "kgts,skd->tkgd", score_grad, key_rot, preferred_element_type=jnp.float32
        ).reshape(row_length, HEADS, HD)
        * scale_factor
    )
    rot_key_grad = (
        jnp.einsum("kgts,tkgd->skd", score_grad, grouped, preferred_element_type=jnp.float32)
        * scale_factor
    )
    cosine, sine_part = rotary_tables(seg_start)
    query_grad = (
        rotate_back(rot_query_grad, cosine, sine_part)
        .reshape(row_length, HEADS * HD)
        .astype(jnp.bfloat16)
    )
    key_grad = (
        rotate_back(rot_key_grad, cosine, sine_part)
        .reshape(row_length, KV_HEADS * HD)
        .astype(jnp.bfloat16)
    )
    attn_grad = (
        times_transposed(query_grad, w_query)
        + times_transposed(key_grad, w_key)
        + times_transposed(value_grad, w_value)
    )
    gain_one_grad = jnp.sum(attn_grad * normed, axis=0)
    scaled_one = attn_grad * gain_one.astype(jnp.float32)
    input_grad = mid_grad + first_inv * (
        scaled_one - normed * jnp.mean(scaled_one * normed, axis=-1, keepdims=True)
    )
    grad_pieces = (query_grad, key_grad, value_grad, out_grad, gate_grad, up_grad, down_grad)
    return (input_grad.astype(jnp.bfloat16), grad_pieces, gain_one_grad, gain_two_grad)


def matrix_terms(kept_rows, pieces):
    attn_rows, attended_rows, ffn_rows, activated_rows = (
        kept_rows[1],
        kept_rows[6],
        kept_rows[8],
        kept_rows[11],
    )
    return (
        across_rows(attn_rows, pieces[0]),
        across_rows(attn_rows, pieces[1]),
        across_rows(attn_rows, pieces[2]),
        across_rows(attended_rows, pieces[3]),
        across_rows(ffn_rows, pieces[4]),
        across_rows(ffn_rows, pieces[5]),
        across_rows(activated_rows, pieces[6]),
    )


def shards(
    tokens,
    cotangent,
    seq_lengths,
    w_query,
    w_key,
    w_value,
    w_out,
    w_gate,
    w_up,
    w_down,
    gain_attn,
    gain_ffn,
):
    section_index = lax.axis_index("pipe")
    row_count = seq_lengths.shape[0]
    row_length = tokens.shape[0] // row_count
    feature_dim = tokens.shape[1]
    kv_width = KV_HEADS * HD
    group_size = HEADS // KV_HEADS
    starts = row_starts(seq_lengths, row_length)
    inputs = tokens.reshape(row_count, row_length, feature_dim)
    cotangents = cotangent.reshape(row_count, row_length, feature_dim)
    gathered = (
        lax.all_gather(w_query, "dp", axis=1, tiled=True),
        lax.all_gather(w_key, "dp", axis=1, tiled=True),
        lax.all_gather(w_value, "dp", axis=1, tiled=True),
        lax.all_gather(w_out, "dp", axis=1, tiled=True),
        lax.all_gather(w_gate, "dp", axis=1, tiled=True),
        lax.all_gather(w_up, "dp", axis=1, tiled=True),
        lax.all_gather(w_down, "dp", axis=1, tiled=True),
        lax.all_gather(gain_attn, "dp", axis=1, tiled=True),
        lax.all_gather(gain_ffn, "dp", axis=1, tiled=True),
    )
    params = tuple((piece[0] for piece in gathered))

    def blank(width_last, dtype_name):
        return jnp.zeros((row_count, row_length, width_last), dtype_name)

    stores = (
        blank(feature_dim, jnp.bfloat16),
        blank(feature_dim, jnp.bfloat16),
        jnp.zeros((row_count, row_length, HEADS, HD), jnp.bfloat16),
        jnp.zeros((row_count, row_length, KV_HEADS, HD), jnp.bfloat16),
        jnp.zeros((row_count, row_length, KV_HEADS, HD), jnp.bfloat16),
        jnp.zeros((row_count, KV_HEADS, group_size, row_length, 1), jnp.float32),
        blank(feature_dim, jnp.bfloat16),
        blank(feature_dim, jnp.float32),
        blank(feature_dim, jnp.bfloat16),
        blank(FF, jnp.float32),
        blank(FF, jnp.float32),
        blank(FF, jnp.bfloat16),
    )
    layer_store = blank(feature_dim, jnp.bfloat16)
    received = blank(feature_dim, jnp.bfloat16)
    piece_store = (
        blank(feature_dim, jnp.bfloat16),
        blank(kv_width, jnp.bfloat16),
        blank(kv_width, jnp.bfloat16),
        blank(feature_dim, jnp.bfloat16),
        blank(FF, jnp.bfloat16),
        blank(FF, jnp.bfloat16),
        blank(feature_dim, jnp.bfloat16),
    )
    gain_sums = (jnp.zeros((feature_dim,), jnp.float32), jnp.zeros((feature_dim,), jnp.float32))
    grad_store = blank(feature_dim, jnp.bfloat16)
    grad_received = blank(feature_dim, jnp.bfloat16)
    shard_sums = None
    for tick_index in range(row_count + 2):
        forward_slot = tick_index - section_index
        forward_active = (forward_slot >= 0) & (forward_slot < row_count)
        forward_row = jnp.clip(forward_slot, 0, row_count - 1)

        def advance(state, which_row=forward_row, received=received):
            kept_stores, out_store = state
            source = jnp.where(section_index == 0, inputs[which_row], received[which_row])
            result, kept_values = forward_unit(params, source, starts[which_row])
            kept_stores = tuple(
                (
                    lax.dynamic_update_index_in_dim(store, item, which_row, 0)
                    for store, item in zip(kept_stores, kept_values)
                )
            )
            out_store = lax.dynamic_update_index_in_dim(out_store, result, which_row, 0)
            return ((kept_stores, out_store), result)

        def standby(state):
            return (state, jnp.zeros((row_length, feature_dim), jnp.bfloat16))

        (stores, layer_store), outgoing = lax.cond(
            forward_active, advance, standby, (stores, layer_store)
        )
        arrived = passed_along(outgoing, "pipe", 1)
        if tick_index < row_count:
            received = received.at[tick_index].set(arrived)
        backward_slot = tick_index - 2 + section_index
        backward_active = (backward_slot >= 0) & (backward_slot < row_count)
        backward_row = jnp.clip(backward_slot, 0, row_count - 1)

        def retreat(state, which_row=backward_row, grad_received=grad_received):
            kept_stores, pieces, in_store = state
            incoming = jnp.where(
                section_index == 1, cotangents[which_row], grad_received[which_row]
            ).astype(jnp.float32)
            kept_row = tuple((store[which_row] for store in kept_stores))
            input_grad, new_pieces, gain_one_grad, gain_two_grad = backward_unit(
                params, kept_row, starts[which_row], incoming
            )
            pieces = tuple(
                (
                    lax.dynamic_update_index_in_dim(store, item, which_row, 0)
                    for store, item in zip(pieces, new_pieces)
                )
            )
            in_store = lax.dynamic_update_index_in_dim(in_store, input_grad, which_row, 0)
            return ((kept_stores, pieces, in_store), (input_grad, gain_one_grad, gain_two_grad))

        def standby_back(state):
            return (
                state,
                (
                    jnp.zeros((row_length, feature_dim), jnp.bfloat16),
                    jnp.zeros((feature_dim,), jnp.float32),
                    jnp.zeros((feature_dim,), jnp.float32),
                ),
            )

        (stores, piece_store, grad_store), (outgoing_grad, gain_one_grad, gain_two_grad) = lax.cond(
            backward_active, retreat, standby_back, (stores, piece_store, grad_store)
        )
        arrived_grad = passed_along(outgoing_grad, "pipe", -1)
        if 1 <= tick_index <= row_count:
            grad_received = grad_received.at[tick_index - 1].set(arrived_grad)
        gain_sums = (gain_sums[0] + gain_one_grad, gain_sums[1] + gain_two_grad)

    def flatten(store):
        return store.reshape(row_count * row_length, store.shape[-1])

    terms = matrix_terms(
        tuple((flatten(store) if store.ndim == 3 else store for store in stores)),
        tuple((flatten(store) for store in piece_store)),
    )
    shard_sums = (
        lax.psum_scatter(terms[0], "dp", scatter_dimension=0, tiled=True),
        lax.psum_scatter(terms[1], "dp", scatter_dimension=0, tiled=True),
        lax.psum_scatter(terms[2], "dp", scatter_dimension=0, tiled=True),
        lax.psum_scatter(terms[3], "dp", scatter_dimension=0, tiled=True),
        lax.psum_scatter(terms[4], "dp", scatter_dimension=0, tiled=True),
        lax.psum_scatter(terms[5], "dp", scatter_dimension=0, tiled=True),
        lax.psum_scatter(terms[6], "dp", scatter_dimension=0, tiled=True),
        lax.psum_scatter(gain_sums[0], "dp", scatter_dimension=0, tiled=True),
        lax.psum_scatter(gain_sums[1], "dp", scatter_dimension=0, tiled=True),
    )
    layer_outputs = layer_store.reshape(1, row_count * row_length, feature_dim)
    input_grads = grad_store.reshape(1, row_count * row_length, feature_dim)
    return (
        layer_outputs,
        input_grads,
        shard_sums[0][None],
        shard_sums[1][None],
        shard_sums[2][None],
        shard_sums[3][None],
        shard_sums[4][None],
        shard_sums[5][None],
        shard_sums[6][None],
        shard_sums[7][None],
        shard_sums[8][None],
    )


def solution(mesh):
    in_specs = (
        P("dp", None),
        P("dp", None),
        P("dp", None),
        P("pipe", "dp", None),
        P("pipe", "dp", None),
        P("pipe", "dp", None),
        P("pipe", "dp", None),
        P("pipe", "dp", None),
        P("pipe", "dp", None),
        P("pipe", "dp", None),
        P("pipe", "dp"),
        P("pipe", "dp"),
    )
    out_specs = (
        P("pipe", "dp", None),
        P("pipe", "dp", None),
        P("pipe", "dp", None),
        P("pipe", "dp", None),
        P("pipe", "dp", None),
        P("pipe", "dp", None),
        P("pipe", "dp", None),
        P("pipe", "dp", None),
        P("pipe", "dp", None),
        P("pipe", "dp"),
        P("pipe", "dp"),
    )
    return jax.shard_map(shards, mesh=mesh, in_specs=in_specs, out_specs=out_specs, check_vma=False)
```

profile of v0, /device:TPU:1, one launch (start us, length us, event | category | flops | bytes accessed | tf_op | source)
XLA Modules:
  0.0 2161.9 jit_solution(16741120801918238085)
XLA Ops:
  13.9 31.3 %all-reduce.7 = (bf16[1536]{0:T(1024)(128)(2,1)S(1)}, bf16[1536]{0:T(1024)(128)(2,1)S(1)}) all-reduce(bf16[1536]{0:T(1024)(128)(2,1)S(1)} %dynamic-update-slice.25, bf16[1536]{0:T(1024)(128)(2,1)S(1)} %dynamic-update-slice.26), channel_id=1, replica_groups=mesh['pipe'=2,'dp'=16] {'dp'}, use_global_device_ids=true, to_apply=%add.2 | all-reduce | flops 3072 | bytes 12288 | tf_op jit(solution)/shard_map/squeeze | solution.py:285
  45.3 9.8 all-gather.10.cloned.1.call-done
  55.2 43.4 %all-gather.12.cloned.1.call-done = bf16[1,1536,768]{2,1,0:T(8,128)(2,1)} async-done(((bf16[1,96,768]{2,1,0:T(8,128)(2,1)}), bf16[1,1536,768]{2,1,0:T(8,128)(2,1)}) %all-gather.12.cloned.1.call-update) | async-done | bytes 2359312 | tf_op jit(solution)/shard_map/all_gather | solution.py:277
  98.6 54.2 %all-gather.8.cloned.1.call-done = bf16[1,1536,1536]{2,1,0:T(8,128)(2,1)} async-done(((bf16[1,96,1536]{2,1,0:T(8,128)(2,1)}), bf16[1,1536,1536]{2,1,0:T(8,128)(2,1)}) %all-gather.8.cloned.1.call-update) | async-done | bytes 4718608 | tf_op jit(solution)/shard_map/all_gather | solution.py:275
  152.7 53.8 %all-gather.14.cloned.1.call-done = bf16[1,1536,1536]{2,1,0:T(8,128)(2,1)} async-done(((bf16[1,96,1536]{2,1,0:T(8,128)(2,1)}), bf16[1,1536,1536]{2,1,0:T(8,128)(2,1)}) %all-gather.14.cloned.1.call-update) | async-done | bytes 4718608 | tf_op jit(solution)/shard_map/all_gather | solution.py:278
  206.6 101.1 %all-gather.16.cloned.1.call-done = bf16[1,1536,4096]{2,1,0:T(8,128)(2,1)} async-done(((bf16[1,96,4096]{2,1,0:T(8,128)(2,1)}), bf16[1,1536,4096]{2,1,0:T(8,128)(2,1)}) %all-gather.16.cloned.1.call-update) | async-done | bytes 12582928 | tf_op jit(solution)/shard_map/all_gather | solution.py:279
  307.7 100.8 %all-gather.18.cloned.1.call-done = bf16[1,1536,4096]{2,1,0:T(8,128)(2,1)} async-done(((bf16[1,96,4096]{2,1,0:T(8,128)(2,1)}), bf16[1,1536,4096]{2,1,0:T(8,128)(2,1)}) %all-gather.18.cloned.1.call-update) | async-done | bytes 12582928 | tf_op jit(solution)/shard_map/all_gather | solution.py:280
  408.6 101.0 %all-gather.20.cloned.1.call-done = bf16[1,4096,1536]{2,1,0:T(8,128)(2,1)} async-done(((bf16[1,256,1536]{2,1,0:T(8,128)(2,1)}), bf16[1,4096,1536]{2,1,0:T(8,128)(2,1)}) %all-gather.20.cloned.1.call-update) | async-done | bytes 12582928 | tf_op jit(solution)/shard_map/all_gather | solution.py:281
  509.5 66.3 %conditional.10 = (bf16[3,128,1536]{2,1,0:T(8,128)(2,1)}, bf16[3,128,1536]{2,1,0:T(8,128)(2,1)}, bf16[3,128,16,96]{1,3,2,0:T(8,128)(2,1)}, bf16[3,128,8,96]{1,3,...) conditional(s32[]{:T(128)} %convert_element_type.1034, ...), branch_computations={%region_2.3_spmd, %region_3.8_spmd} | conditional | flops 6760455680 | bytes 289016320 | solution.py:340
  510.7 6.6 copy.220
  577.1 8.8 collective-permute-done
  587.0 71.0 %conditional.11 = (bf16[3,128,1536]{2,1,0:T(8,128)(2,1)S(1)}, bf16[3,128,1536]{2,1,0:T(8,128)(2,1)}, bf16[3,128,16,96]{1,3,2,0:T(8,128)(2,1)}, bf16[3,128,8,96]{...) conditional(s32[]{:T(128)} %convert_element_type.1033, ...), branch_computations={%region_8.9_spmd, %region_9.14_spmd} | conditional | flops 6759276032 | bytes 331128448 | solution.py:340
  588.3 6.7 copy.224
  621.9 6.7 copy.329
  631.8 6.3 copy.330
  662.8 11.0 conditional.15
  682.2 55.2 %conditional.12 = (bf16[3,128,1536]{2,1,0:T(8,128)(2,1)S(1)}, bf16[3,128,1536]{2,1,0:T(8,128)(2,1)}, bf16[3,128,16,96]{1,3,2,0:T(8,128)(2,1)}, bf16[3,128,8,96]{...) conditional(s32[]{:T(128)} %convert_element_type.1032, ...), branch_computations={%region_14.15_spmd, %region_15.20_spmd} | conditional | flops 6759276032 | bytes 216614224 | solution.py:340
  684.8 6.7 copy.228
  717.6 8.2 bitcast_dynamic-update-slice_fusion.17
  737.3 53.7 %collective-permute-start.2 = (bf16[128,1536]{1,0:T(8,128)(2,1)}, bf16[128,1536]{1,0:T(8,128)(2,1)}, u32[]{:S(2)}, u32[]{:S(2)}) collective-permute-start(bf16[128,1536]{1,0:T(8,128)(2,1)} %get-tuple-element.1671), channel_id=1, source_target_pairs={{0,16},{1,17},{2,18},{3,19},{4,20},{5,21},{6,22},{7,23},{8,24},{9,... | collective-permute-start | bytes 1179656 | tf_op jit(solution)/shard_map/ppermute | solution.py:21
  793.1 52.2 %conditional.17 = (bf16[3,128,1536]{1,2,0:T(8,128)(2,1)}, bf16[3,128,768]{1,2,0:T(8,128)(2,1)}, bf16[3,128,768]{1,2,0:T(8,128)(2,1)}, bf16[3,128,1536]{2,1,0:T(8...) conditional(s32[]{:T(128)} %convert_element_type.1037, ...), branch_computations={%region_50.51_spmd, %region_51.59_spmd} | conditional | flops 6915280896 | bytes 164718912 | solution.py:378
  795.1 11.4 bitcast_dynamic-update-slice_fusion.45
  806.5 9.0 fusion.385
  815.8 9.7 multiply_reduce_fusion.12
  848.5 8.5 collective-permute-done.4
  858.8 52.0 %conditional.18 = (bf16[3,128,1536]{1,2,0:T(8,128)(2,1)}, bf16[3,128,768]{1,2,0:T(8,128)(2,1)}, bf16[3,128,768]{1,2,0:T(8,128)(2,1)}, bf16[3,128,1536]{2,1,0:T(8...) conditional(s32[]{:T(128)} %convert_element_type.1036, ...), branch_computations={%region_59.60_spmd, %region_60.68_spmd} | conditional | flops 6915280896 | bytes 164718912 | solution.py:378
  860.8 11.5 bitcast_dynamic-update-slice_fusion.49
  872.2 9.0 fusion.387
  881.5 9.7 multiply_reduce_fusion.15
  912.1 56.8 %collective-permute-done.5 = bf16[128,1536]{1,0:T(8,128)(2,1)} collective-permute-done((bf16[128,1536]{1,0:T(8,128)(2,1)}, bf16[128,1536]{1,0:T(8,128)(2,1)}, u32[]{:S(2)}, u32[]{:S(2)}) %collective-permute-start.5) | collective-permute-done | bytes 393248 | tf_op jit(solution)/shard_map/ppermute | solution.py:21
  968.9 54.3 %conditional.19 = (bf16[3,128,1536]{1,2,0:T(8,128)(2,1)}, bf16[3,128,768]{1,2,0:T(8,128)(2,1)}, bf16[3,128,768]{1,2,0:T(8,128)(2,1)}, bf16[3,128,1536]{2,1,0:T(8...) conditional(s32[]{:T(128)} %convert_element_type.1035, ...), branch_computations={%region_68.69_spmd, %region_69.77_spmd} | conditional | flops 6915280896 | bytes 165112112 | solution.py:378
  972.8 11.5 bitcast_dynamic-update-slice_fusion.53
  984.3 9.0 fusion.389
  993.6 9.7 multiply_reduce_fusion.18
  1023.2 5.0 convolution_bitcast_fusion.20
  1028.3 5.0 convolution_bitcast_fusion.21
  1033.3 8.1 convolution_bitcast_fusion.18
  1041.5 8.1 convolution_bitcast_fusion.19
  1049.7 13.8 convolution_bitcast_fusion.15
  1063.8 13.9 convolution_bitcast_fusion.16
  1077.7 13.7 convolution_bitcast_fusion.17
  1093.0 54.7 %all-reduce.6 = (f32[1536]{0:T(1024)S(1)}, f32[1536]{0:T(1024)S(1)}) all-reduce(f32[1536]{0:T(1024)S(1)} %get-tuple-element.2736, f32[1536]{0:T(1024)S(1)} %get-tuple-element.2735), channel_id=9, replica_groups=mesh['pipe'=2,'dp'=16] {'dp'}, use_global_device_ids=true, to_apply=%region_84.85.clone | all-reduce | flops 3072 | bytes 24576
  1148.8 31.8 %reduce-scatter.10.cloned.1.call-done = f32[96,768]{1,0:T(8,128)} async-done(((f32[1536,768]{1,0:T(8,128)}), f32[96,768]{1,0:T(8,128)}) %reduce-scatter.10.cloned.1.call-update) | async-done | bytes 294928 | tf_op jit(solution)/shard_map/reduce_scatter | solution.py:395
  1180.6 116.5 %reduce-scatter.14.cloned.1.call-done = f32[96,1536]{1,0:T(8,128)} async-done(((f32[1536,1536]{1,0:T(8,128)}), f32[96,1536]{1,0:T(8,128)}) %reduce-scatter.14.cloned.1.call-update) | async-done | bytes 589840 | tf_op jit(solution)/shard_map/reduce_scatter | solution.py:397
  1297.1 115.6 %reduce-scatter.8.cloned.1.call-done = f32[96,1536]{1,0:T(8,128)} async-done(((f32[1536,1536]{1,0:T(8,128)}), f32[96,1536]{1,0:T(8,128)}) %reduce-scatter.8.cloned.1.call-update) | async-done | bytes 589840 | tf_op jit(solution)/shard_map/reduce_scatter | solution.py:394
  1412.7 248.0 %reduce-scatter.20.cloned.1.call-done = f32[256,1536]{1,0:T(8,128)} async-done(((f32[4096,1536]{1,0:T(8,128)}), f32[256,1536]{1,0:T(8,128)}) %reduce-scatter.20.cloned.1.call-update) | async-done | bytes 1572880 | tf_op jit(solution)/shard_map/reduce_scatter | solution.py:400
  1660.6 247.3 %reduce-scatter.18.cloned.1.call-done = f32[96,4096]{1,0:T(8,128)} async-done(((f32[1536,4096]{1,0:T(8,128)}), f32[96,4096]{1,0:T(8,128)}) %reduce-scatter.18.cloned.1.call-update) | async-done | bytes 1572880 | tf_op jit(solution)/shard_map/reduce_scatter | solution.py:399
  1908.0 247.2 %reduce-scatter.16.cloned.1.call-done = f32[96,4096]{1,0:T(8,128)} async-done(((f32[1536,4096]{1,0:T(8,128)}), f32[96,4096]{1,0:T(8,128)}) %reduce-scatter.16.cloned.1.call-update) | async-done | bytes 1572880 | tf_op jit(solution)/shard_map/reduce_scatter | solution.py:398
  (550 shorter events, 264.6 us)
Async XLA Ops:
  7.2 48.0 %all-gather.10.cloned.1.call-start = ((), (), s32[]{:S(2)}) async-start(), calls=%async_computation.8 | async-start | bytes 2506752 | tf_op jit(solution)/shard_map/all_gather | solution.py:276
  8.0 90.6 %all-gather.12.cloned.1.call-start = ((), (), s32[]{:S(2)}) async-start(), calls=%async_computation.9 | async-start | bytes 2506752 | tf_op jit(solution)/shard_map/all_gather | solution.py:277
  8.7 144.0 %all-gather.8.cloned.1.call-start = ((), (), s32[]{:S(2)}) async-start(), calls=%async_computation.7 | async-start | bytes 5013504 | tf_op jit(solution)/shard_map/all_gather | solution.py:275
  9.4 197.1 %all-gather.14.cloned.1.call-start = ((), (), s32[]{:S(2)}) async-start(), calls=%async_computation.10 | async-start | bytes 5013504 | tf_op jit(solution)/shard_map/all_gather | solution.py:278
  10.0 297.7 %all-gather.16.cloned.1.call-start = ((), (), s32[]{:S(2)}) async-start(), calls=%async_computation.11 | async-start | bytes 13369344 | tf_op jit(solution)/shard_map/all_gather | solution.py:279
  10.6 398.0 %all-gather.18.cloned.1.call-start = ((), (), s32[]{:S(2)}) async-start(), calls=%async_computation.12 | async-start | bytes 13369344 | tf_op jit(solution)/shard_map/all_gather | solution.py:280
  11.2 498.4 %all-gather.20.cloned.1.call-start = ((), (), s32[]{:S(2)}) async-start(), calls=%async_computation.13 | async-start | bytes 13369344 | tf_op jit(solution)/shard_map/all_gather | solution.py:281
  11.9 1136.9 %reduce-scatter.12.cloned.1.call-start = ((), (), s32[]{:S(2)}) async-start(), calls=%async_computation.16 | async-start | bytes 5013504 | tf_op jit(solution)/shard_map/reduce_scatter | solution.py:396
  45.3 540.7 %copy-start.133 = (s32[3,128]{1,0:T(4,128)}, s32[3,128]{1,0:T(4,128)S(1)}, u32[]{:S(2)}) copy-start(s32[3,128]{1,0:T(4,128)S(1)} %select_reduce_fusion) | copy-start | bytes 4612
  529.0 10.5 slice-start.49
  536.0 11.3 slice-start.6
  539.4 7.8 slice-start.7
  543.3 10.5 slice-start
  550.4 11.4 slice-start.24
  553.8 7.9 slice-start.25
  553.8 7.9 slice-start.26
  575.8 10.1 collective-permute-start
  588.2 29.0 %copy-start.27 = (bf16[1,128,1536]{2,1,0:T(8,128)(2,1)}, bf16[1,128,1536]{2,1,0:T(8,128)(2,1)S(1)}, u32[]{:S(2)}) copy-start(bf16[1,128,1536]{2,1,0:T(8,128)(2,1)S(1)} %get-tuple-element.2484) | copy-start | bytes 1179652 | tf_op jit(solution)/shard_map/cond
  588.3 23.4 %copy-start.135 = (f32[128]{0:T(128)}, f32[128]{0:T(128)S(1)}, u32[]{:S(2)}) copy-start(f32[128]{0:T(128)S(1)} %add_rsqrt_fusion.3) | copy-start | bytes 1540 | tf_op jit(solution)/shard_map/cond
  605.6 9.4 copy-start.114
  606.7 8.3 copy-start.116
  617.2 11.3 slice-start.3
  618.3 10.3 slice-start.4
  628.6 9.5 slice-start.9
  628.6 9.5 slice-start.10
  658.0 22.4 %collective-permute-start.1 = (bf16[128,1536]{1,0:T(8,128)(2,1)}, bf16[128,1536]{1,0:T(8,128)(2,1)}, u32[]{:S(2)}, u32[]{:S(2)}) collective-permute-start(bf16[128,1536]{1,0:T(8,128)(2,1)} %get-tuple-element.1657), channel_id=1, source_target_pairs={{0,16},{1,17},{2,18},{3,19},{4,20},{5,21},{6,22},{7,23},{8,24},{9,... | collective-permute-start | bytes 1179656 | tf_op jit(solution)/shard_map/ppermute | solution.py:21
  679.1 111.9 %collective-permute-start.3 = (bf16[128,1536]{1,0:T(8,128)(2,1)}, bf16[128,1536]{1,0:T(8,128)(2,1)}, u32[]{:S(2)}, u32[]{:S(2)}) collective-permute-start(bf16[128,1536]{1,0:T(8,128)(2,1)} %get-tuple-element.1702), channel_id=1, source_target_pairs={{16,0},{17,1},{18,2},{19,3},{20,4},{21,5},{22,6},{23,7},{24,8},{25... | collective-permute-start | bytes 1179656 | tf_op jit(solution)/shard_map/ppermute | solution.py:21
  716.5 9.4 slice-start.15
  717.6 8.3 slice-start.16
  717.6 8.3 slice-start.17
  737.3 109.2 %collective-permute-start.2 = (bf16[128,1536]{1,0:T(8,128)(2,1)}, bf16[128,1536]{1,0:T(8,128)(2,1)}, u32[]{:S(2)}, u32[]{:S(2)}) collective-permute-start(bf16[128,1536]{1,0:T(8,128)(2,1)} %get-tuple-element.1671), channel_id=1, source_target_pairs={{0,16},{1,17},{2,18},{3,19},{4,20},{5,21},{6,22},{7,23},{8,24},{9,... | collective-permute-start | bytes 1179656 | tf_op jit(solution)/shard_map/ppermute | solution.py:21
  806.5 9.0 copy-start.22
  815.8 11.7 slice-start.55
  815.8 11.7 slice-start.56
  845.3 11.8 collective-permute-start.4
  872.2 9.0 copy-start.23
  881.5 11.7 slice-start.57
  881.5 11.7 slice-start.58
  910.8 58.1 %collective-permute-start.5 = (bf16[128,1536]{1,0:T(8,128)(2,1)}, bf16[128,1536]{1,0:T(8,128)(2,1)}, u32[]{:S(2)}, u32[]{:S(2)}) collective-permute-start(bf16[128,1536]{1,0:T(8,128)(2,1)} %get-tuple-element.1724), channel_id=1, source_target_pairs={{16,0},{17,1},{18,2},{19,3},{20,4},{21,5},{22,6},{23,7},{24,8},{25... | collective-permute-start | bytes 1179656 | tf_op jit(solution)/shard_map/ppermute | solution.py:21
  984.3 9.0 copy-start.24
  993.5 11.7 slice-start.59
  993.6 11.7 slice-start.60
  1028.2 152.4 %reduce-scatter.10.cloned.1.call-start = ((), (), s32[]{:S(2)}) async-start(), calls=%async_computation.15 | async-start | bytes 5013504 | tf_op jit(solution)/shard_map/reduce_scatter | solution.py:395
  1033.2 263.9 %reduce-scatter.14.cloned.1.call-start = ((), (), s32[]{:S(2)}) async-start(), calls=%async_computation.17 | async-start | bytes 10027008 | tf_op jit(solution)/shard_map/reduce_scatter | solution.py:397
  1041.4 371.3 %reduce-scatter.8.cloned.1.call-start = ((), (), s32[]{:S(2)}) async-start(), calls=%async_computation.14 | async-start | bytes 10027008 | tf_op jit(solution)/shard_map/reduce_scatter | solution.py:394
  1049.6 611.0 %reduce-scatter.20.cloned.1.call-start = ((), (), s32[]{:S(2)}) async-start(), calls=%async_computation.20 | async-start | bytes 26738688 | tf_op jit(solution)/shard_map/reduce_scatter | solution.py:400
  1063.5 844.5 %reduce-scatter.18.cloned.1.call-start = ((), (), s32[]{:S(2)}) async-start(), calls=%async_computation.19 | async-start | bytes 26738688 | tf_op jit(solution)/shard_map/reduce_scatter | solution.py:399
  1077.7 1077.5 %reduce-scatter.16.cloned.1.call-start = ((), (), s32[]{:S(2)}) async-start(), calls=%async_computation.18 | async-start | bytes 26738688 | tf_op jit(solution)/shard_map/reduce_scatter | solution.py:398
  (97 other events, 335.7 us)
Sparse Core Ops, SparseCore 0:
  10.3 44.8 all-gather.9
  57.5 41.0 all-gather.11
  100.8 51.8 all-gather.7
  154.9 51.6 all-gather.13
  208.7 98.9 all-gather.15
  309.9 98.6 all-gather.17
  410.8 98.6 all-gather.19
  1028.3 72.8 reduce-scatter.11
  1105.7 74.9 reduce-scatter.9
  1185.2 111.8 reduce-scatter.13
  1301.8 110.8 reduce-scatter.7
  1417.2 243.3 reduce-scatter.19
  1665.3 242.6 reduce-scatter.17
  1912.5 242.6 reduce-scatter.15
where the time goes:
time: 2170 us; the launch traced here: 2160 us
  waiting for transfers between devices  1550 us (71%)
  matrix products  262 us (12%)
  local copies, waits for them, and re-layouts  138 us (6%)
  blocking collectives  85.9 us (4%)
  starting transfers between devices  64.4 us (3%)
  other arithmetic  44.6 us (2%)
    reduce_scatter x1, waiting for transfers between devices, shards(): lax.psum_scatter(terms[6], 'dp', scatter_dimension=0, tiled=True)  248 us
    reduce_scatter x1, waiting for transfers between devices, shards(): lax.psum_scatter(terms[5], 'dp', scatter_dimension=0, tiled=True)  247 us
    reduce_scatter x1, waiting for transfers between devices, shards(): lax.psum_scatter(terms[4], 'dp', scatter_dimension=0, tiled=True)  247 us
    reduce_scatter x1, waiting for transfers between devices, shards(): lax.psum_scatter(terms[3], 'dp', scatter_dimension=0, tiled=True)  116 us
    reduce_scatter x1, waiting for transfers between devices, shards(): lax.psum_scatter(terms[0], 'dp', scatter_dimension=0, tiled=True)  116 us
    dot_general x21, matrix products, times_transposed(): lax.dot_general(first_operand, second_operand, (((1,), (1,)), ((), ())),...  107 us
    all_gather x1, waiting for transfers between devices, shards(): lax.all_gather(w_gate, 'dp', axis=1, tiled=True)  101 us
    all_gather x1, waiting for transfers between devices, shards(): lax.all_gather(w_down, 'dp', axis=1, tiled=True)  101 us
  transfers between devices with their start and end apart: 20, of which 16 were waited for; matrix products, arithmetic and copies ran while one was open for 9% of the time, Pallas kernels for 0%

commit v1 on v0

v1 whole, which is shorter than its diff:
```python
import functools, math
import jax
import jax.numpy as jnp
from jax import lax
from jax.experimental import pallas as pl
from jax.experimental.pallas import tpu as pltpu
from jax.sharding import PartitionSpec as P

MESH = pl.DeviceIdType.MESH
DEPTH = 4


def ring_place(dp_index, chips):
    inner = chips // DEPTH
    core = dp_index % 2
    chip = dp_index // 2
    deep = chip // inner
    spot = chip % inner
    half = inner // 2
    turn = spot + (spot // half) * (3 * half - 1 - 2 * spot)
    return turn * DEPTH + deep + (turn % 2) * (DEPTH - 1 - 2 * deep), core


def ring_device(place, core, chips):
    inner = chips // DEPTH
    half = inner // 2
    turn = place // DEPTH
    step = place % DEPTH
    deep = step + (turn % 2) * (DEPTH - 1 - 2 * step)
    spot = turn + (turn // half) * (3 * half - 1 - 2 * turn)
    return (deep * inner + spot) * 2 + core


def gather_kernel(chips, count, *refs):
    shards = refs[:count]
    wholes = refs[count : 2 * count]
    stages = refs[2 * count : 3 * count]
    ring_send, ring_recv, pair_send, pair_recv, own_pair, own_load = refs[3 * count :]
    me = lax.axis_index("dp")
    place, core = ring_place(me, chips)
    right = ring_device((place + 1) % chips, core, chips)
    left = ring_device((place + chips - 1) % chips, core, chips)
    partner = me + 1 - 2 * core
    barrier = pltpu.get_barrier_semaphore()
    for other in (right, left, partner):
        pl.semaphore_signal(barrier, inc=1, device_id={"dp": other}, device_id_type=MESH)
    pl.semaphore_wait(barrier, 3)

    def block(index, owner, way):
        rows, columns = shards[index].shape
        return wholes[index].at[
            pl.ds(pl.multiple_of(owner * rows, 8), rows), pl.ds(way * (columns // 2), columns // 2)
        ]

    def ring_copy(index, way, step, source=None):
        owner_place = (place + chips - step) % chips if way == 0 else (place + step) % chips
        owner = ring_device(owner_place, core, chips)
        target = block(index, owner, way)
        return pltpu.make_async_remote_copy(
            src_ref=target if source is None else source,
            dst_ref=target,
            send_sem=ring_send.at[index, way, step],
            recv_sem=ring_recv.at[index, way, step],
            device_id={"dp": (right, left)[way]},
            device_id_type=MESH,
        )

    def arrived(index, way, step):
        owner_place = (place + chips - step - 1) % chips if way == 0 else (place + step + 1) % chips
        owner = ring_device(owner_place, core, chips)
        target = block(index, owner, way)
        ring = pltpu.make_async_remote_copy(
            src_ref=target, dst_ref=target,
            send_sem=ring_send.at[index, way, step], recv_sem=ring_recv.at[index, way, step],
            device_id={"dp": (right, left)[way]}, device_id_type=MESH,
        )
        pair = pltpu.make_async_remote_copy(
            src_ref=target, dst_ref=target,
            send_sem=pair_send.at[index, way, step], recv_sem=pair_recv.at[index, way, step],
            device_id={"dp": partner}, device_id_type=MESH,
        )
        return ring, pair

    def own_pair_copy(index, device):
        rows = shards[index].shape[0]
        return pltpu.make_async_remote_copy(
            src_ref=shards[index],
            dst_ref=wholes[index].at[pl.ds(pl.multiple_of(device * rows, 8), rows), :],
            send_sem=own_pair.at[0, index], recv_sem=own_pair.at[1, index],
            device_id={"dp": partner}, device_id_type=MESH,
        )

    for index in range(count):
        columns = shards[index].shape[1]
        for way in range(2):
            ring_copy(index, way, 0, shards[index].at[:, pl.ds(way * (columns // 2), columns // 2)]).start()
    loads = []
    for index in range(count):
        own_pair_copy(index, me).start()
        loads.append(pltpu.make_async_copy(shards[index], stages[index], own_load.at[0, index]))
        loads[-1].start()
    stores = []
    for index in range(count):
        rows = shards[index].shape[0]
        loads[index].wait()
        stores.append(
            pltpu.make_async_copy(
                stages[index],
                wholes[index].at[pl.ds(pl.multiple_of(me * rows, 8), rows), :],
                own_load.at[1, index],
            )
        )
        stores[-1].start()

    def hop(step, carry):
        for index in range(count):
            for way in range(2):
                ring, pair = arrived(index, way, step - 1)
                ring.wait_recv()
                ring_copy(index, way, step).start()
                pair.start()
        return carry

    lax.fori_loop(1, chips - 1, hop, 0)
    for index in range(count):
        for way in range(2):
            ring, pair = arrived(index, way, chips - 2)
            ring.wait_recv()
            pair.start()

    def finish(step, carry):
        for index in range(count):
            for way in range(2):
                ring, pair = arrived(index, way, step)
                ring.wait_send()
                pair.wait_send()
                pair.wait_recv()
        return carry

    lax.fori_loop(0, chips - 1, finish, 0)
    for index in range(count):
        own_pair_copy(index, me).wait_send()
        own_pair_copy(index, partner).wait_recv()
        stores[index].wait()


def gathered(shards, chips):
    count = len(shards)
    steps = chips - 1
    return pl.pallas_call(
        functools.partial(gather_kernel, chips, count),
        out_shape=[jax.ShapeDtypeStruct((s.shape[0] * 2 * chips, s.shape[1]), s.dtype) for s in shards],
        in_specs=[pl.BlockSpec(memory_space=pl.ANY)] * count,
        out_specs=[pl.BlockSpec(memory_space=pl.ANY)] * count,
        scratch_shapes=[pltpu.VMEM(s.shape, s.dtype) for s in shards]
        + [
            pltpu.SemaphoreType.DMA((count, 2, steps)),
            pltpu.SemaphoreType.DMA((count, 2, steps)),
            pltpu.SemaphoreType.DMA((count, 2, steps)),
            pltpu.SemaphoreType.DMA((count, 2, steps)),
            pltpu.SemaphoreType.DMA((2, count)),
            pltpu.SemaphoreType.DMA((2, count)),
        ],
        compiler_params=pltpu.CompilerParams(collective_id=0, has_side_effects=True),
        name="gather_weights",
    )(*shards)


def scatter_kernel(chips, count, *refs):
    grads = refs[:count]
    sums = refs[count : 2 * count]
    lands = refs[2 * count : 3 * count]
    rest = refs[3 * count :]
    firsts = rest[:count]
    arrivals = rest[count : 2 * count]
    owns = rest[2 * count : 3 * count]
    mates = rest[3 * count : 4 * count]
    ring_send, ring_recv, pair_send, pair_recv, own_load, mate_load = rest[4 * count :]
    me = lax.axis_index("dp")
    place, core = ring_place(me, chips)
    right = ring_device((place + 1) % chips, core, chips)
    left = ring_device((place + chips - 1) % chips, core, chips)
    partner = me + 1 - 2 * core
    barrier = pltpu.get_barrier_semaphore()
    for other in (right, left, partner):
        pl.semaphore_signal(barrier, inc=1, device_id={"dp": other}, device_id_type=MESH)
    pl.semaphore_wait(barrier, 3)

    def owner_chip(way, step):
        return (place + 2 * chips - 1 - step) % chips if way == 0 else (place + 1 + step) % chips

    def pair_copy(index, way, step):
        _, _, rows, columns = arrivals[index].shape
        source = ring_device(owner_chip(way, step), 1 - core, chips)
        return pltpu.make_async_remote_copy(
            src_ref=grads[index].at[
                pl.ds(pl.multiple_of(source * rows, 8), rows), pl.ds(way * columns, columns)
            ],
            dst_ref=lands[index].at[way, step],
            send_sem=pair_send.at[index, way, step],
            recv_sem=pair_recv.at[index, way, step],
            device_id={"dp": partner},
            device_id_type=MESH,
        )

    def own_copy(index, way, step):
        _, _, rows, columns = arrivals[index].shape
        mine = ring_device(owner_chip(way, step), core, chips)
        return pltpu.make_async_copy(
            grads[index].at[
                pl.ds(pl.multiple_of(mine * rows, 8), rows), pl.ds(way * columns, columns)
            ],
            owns[index].at[step % 2, way],
            own_load.at[index, way, step % 2],
        )

    def mate_copy(index, way, step):
        return pltpu.make_async_copy(
            lands[index].at[way, step], mates[index].at[step % 2, way], mate_load.at[index, way, step % 2]
        )

    def ring_copy(index, way, step, source):
        return pltpu.make_async_remote_copy(
            src_ref=source,
            dst_ref=arrivals[index].at[way, step],
            send_sem=ring_send.at[index, way, step],
            recv_sem=ring_recv.at[index, way, step],
            device_id={"dp": (right, left)[way]},
            device_id_type=MESH,
        )

    def start_pair(step, carry):
        for index in range(count):
            for way in range(2):
                pair_copy(index, way, step).start()
        return carry

    lax.fori_loop(0, chips, start_pair, 0)

    def fetch(step):
        for index in range(count):
            for way in range(2):
                own_copy(index, way, step).start()
                pair_copy(index, way, step).wait_recv()
                mate_copy(index, way, step).start()

    def added(index, way, step, extra, target, kind):
        _, _, rows, columns = arrivals[index].shape
        own_copy(index, way, step).wait()
        mate_copy(index, way, step).wait()
        part = 32 if rows % 32 == 0 else 8
        slot = step % 2

        def piece(at, carry):
            band = pl.ds(pl.multiple_of(at * part, part), part)
            value = owns[index][slot, way, band, :].astype(jnp.float32) + mates[index][
                slot, way, band, :
            ].astype(jnp.float32)
            if extra is not None:
                value = value + extra[band, :].astype(jnp.float32)
            target[band, :] = value.astype(kind)
            return carry

        lax.fori_loop(0, rows // part, piece, 0)

    fetch(0)
    fetch(1)
    for index in range(count):
        for way in range(2):
            added(index, way, 0, None, firsts[index].at[way], firsts[index].dtype)
        for way in range(2):
            ring_copy(index, way, 0, firsts[index].at[way]).start()

    def hop(step, carry):
        fetch(step + 1)
        for index in range(count):
            for way in range(2):
                here = arrivals[index].at[way, step - 1]
                ring_copy(index, way, step - 1, here).wait_recv()
                added(index, way, step, here, here, here.dtype)
            for way in range(2):
                ring_copy(index, way, step, arrivals[index].at[way, step - 1]).start()
        return carry

    lax.fori_loop(1, chips - 1, hop, 0)
    for index in range(count):
        _, _, rows, columns = arrivals[index].shape
        for way in range(2):
            here = arrivals[index].at[way, chips - 2]
            ring_copy(index, way, chips - 2, here).wait_recv()
            added(
                index, way, chips - 1, here, sums[index].at[:, pl.ds(way * columns, columns)], jnp.float32
            )

    def finish(step, carry):
        for index in range(count):
            for way in range(2):
                ring_copy(index, way, step, firsts[index].at[way]).wait_send()
        return carry

    lax.fori_loop(0, chips - 1, finish, 0)

    def finish_pair(step, carry):
        for index in range(count):
            for way in range(2):
                pair_copy(index, way, step).wait_send()
        return carry

    lax.fori_loop(0, chips, finish_pair, 0)


def scattered(grads, chips):
    count = len(grads)
    steps = chips - 1
    half = [(g.shape[0] // (2 * chips), g.shape[1] // 2) for g in grads]
    kinds = [g.dtype for g in grads]
    outs = pl.pallas_call(
        functools.partial(scatter_kernel, chips, count),
        out_shape=[jax.ShapeDtypeStruct((r, 2 * c), jnp.float32) for r, c in half]
        + [jax.ShapeDtypeStruct((2, chips, r, c), k) for (r, c), k in zip(half, kinds)],
        in_specs=[pl.BlockSpec(memory_space=pl.ANY)] * count,
        out_specs=[pl.BlockSpec(memory_space=pltpu.VMEM)] * count
        + [pl.BlockSpec(memory_space=pl.ANY)] * count,
        scratch_shapes=[pltpu.VMEM((2, r, c), k) for (r, c), k in zip(half, kinds)]
        + [pltpu.VMEM((2, steps, r, c), k) for (r, c), k in zip(half, kinds)]
        + [pltpu.VMEM((2, 2, r, c), k) for (r, c), k in zip(half, kinds)]
        + [pltpu.VMEM((2, 2, r, c), k) for (r, c), k in zip(half, kinds)]
        + [
            pltpu.SemaphoreType.DMA((count, 2, steps)),
            pltpu.SemaphoreType.DMA((count, 2, steps)),
            pltpu.SemaphoreType.DMA((count, 2, chips)),
            pltpu.SemaphoreType.DMA((count, 2, chips)),
            pltpu.SemaphoreType.DMA((count, 2, 2)),
            pltpu.SemaphoreType.DMA((count, 2, 2)),
        ],
        compiler_params=pltpu.CompilerParams(
            collective_id=1, has_side_effects=True, vmem_limit_bytes=60 << 20
        ),
        name="scatter_grads",
    )(*grads)
    return outs[:count]


HEADS = 16
KV_HEADS = 8
HD = 96
GROUP = HEADS // KV_HEADS
EPSILON = 1e-05
ROPE_BASE = 100000.0
SCALE = 1.0 / math.sqrt(HD)
GAIN_LANES = 128


def passed_along(array, axis, by):
    count = lax.axis_size(axis)
    pairs = [(i, i + by) for i in range(count) if 0 <= i + by < count]
    return lax.ppermute(array, axis, pairs)


def row_starts(lengths, row_length):
    seq_ends = jnp.cumsum(lengths, axis=-1)
    slot_ids = jnp.arange(row_length, dtype=jnp.int32)
    reached = jnp.where(seq_ends[:, None, :] <= slot_ids[None, :, None], seq_ends[:, None, :], 0)
    return jnp.max(reached, axis=-1)


def rotary_tables(starts):
    row_length = starts.shape[1]
    half_dim = HD // 2
    places = (jnp.arange(row_length, dtype=jnp.int32)[None] - starts).astype(jnp.float32)
    inv_freqs = jnp.exp(jnp.arange(half_dim, dtype=jnp.float32) * (-2.0 * math.log(ROPE_BASE) / HD))
    angles = places[:, :, None] * inv_freqs[None, None, :]
    return (jnp.cos(angles)[:, :, None, :], jnp.sin(angles)[:, :, None, :])


def rotate(operand, cosine, sine_part):
    half_dim = operand.shape[-1] // 2
    front_half, back_half = (operand[..., :half_dim], operand[..., half_dim:])
    return jnp.concatenate(
        [front_half * cosine - back_half * sine_part, back_half * cosine + front_half * sine_part],
        axis=-1,
    )


def attend_mask(starts):
    row_length = starts.shape[1]
    slot_ids = jnp.arange(row_length, dtype=jnp.int32)
    same = starts[:, None, :] == starts[:, :, None]
    return same & (slot_ids[None, None, :] <= slot_ids[None, :, None])


def inv_rms(operand):
    return lax.rsqrt(jnp.mean(operand * operand, axis=-1, keepdims=True) + EPSILON)


def times(first_operand, second_operand):
    return jnp.dot(first_operand, second_operand, preferred_element_type=jnp.float32)


def times_transposed(first_operand, second_operand):
    return lax.dot_general(
        first_operand, second_operand, (((1,), (1,)), ((), ())), preferred_element_type=jnp.float32
    )


def across_rows(first_operand, second_operand):
    return lax.dot_general(
        first_operand, second_operand, (((0,), (0,)), ((), ())), preferred_element_type=jnp.float32
    ).astype(jnp.bfloat16)


def mixed(spec, first_operand, second_operand):
    return jnp.einsum(spec, first_operand, second_operand, preferred_element_type=jnp.float32)


def scores_of(query_rot, key_rot, mask):
    raw_scores = mixed("rtkgd,rskd->rkgts", query_rot, key_rot) * SCALE
    return jnp.where(mask[:, None, None], raw_scores, -1e30)


def forward_unit(params, input_low, tables, mask):
    w_query, w_key, w_value, w_out, w_gate, w_up, w_down, gain_one, gain_two = params
    rows, row_length = mask.shape[:2]
    tokens = input_low.shape[0]
    hidden = input_low.astype(jnp.float32)
    normed = hidden * inv_rms(hidden)
    attn_input = (normed * gain_one).astype(jnp.bfloat16)
    cosine, sine_part = tables
    query_proj = times(attn_input, w_query).reshape(rows, row_length, HEADS, HD)
    key_proj = times(attn_input, w_key).reshape(rows, row_length, KV_HEADS, HD)
    value_proj = times(attn_input, w_value).reshape(rows, row_length, KV_HEADS, HD)
    query_rot = rotate(query_proj, cosine, sine_part).astype(jnp.bfloat16)
    query_rot = query_rot.reshape(rows, row_length, KV_HEADS, GROUP, HD)
    key_rot = rotate(key_proj, cosine, sine_part).astype(jnp.bfloat16)
    value_low = value_proj.astype(jnp.bfloat16)
    scores = scores_of(query_rot, key_rot, mask)
    row_max = jnp.max(scores, axis=-1, keepdims=True)
    exp_scores = jnp.exp(scores - row_max)
    exp_total = jnp.sum(exp_scores, axis=-1, keepdims=True)
    log_total = row_max + jnp.log(exp_total)
    probs_low = (exp_scores / exp_total).astype(jnp.bfloat16)
    attended = mixed("rkgts,rskd->rtkgd", probs_low, value_low)
    attended = attended.reshape(tokens, HEADS * HD).astype(jnp.bfloat16)
    mid_stream = hidden + times(attended, w_out)
    normed_two = mid_stream * inv_rms(mid_stream)
    ffn_input = (normed_two * gain_two).astype(jnp.bfloat16)
    gate_proj = times(ffn_input, w_gate)
    up_proj = times(ffn_input, w_up)
    activated = (jax.nn.silu(gate_proj) * up_proj).astype(jnp.bfloat16)
    result = mid_stream + times(activated, w_down)
    kept_values = (
        input_low, attn_input, query_rot, key_rot, value_low, log_total, attended, mid_stream,
        ffn_input, gate_proj.astype(jnp.bfloat16), up_proj.astype(jnp.bfloat16), activated,
    )
    return (result.astype(jnp.bfloat16), kept_values)


def backward_unit(params, kept_values, tables, mask, incoming_low):
    w_query, w_key, w_value, w_out, w_gate, w_up, w_down, gain_one, gain_two = params
    (
        input_low, attn_input, query_rot, key_rot, value_low, log_total, attended, mid_stream,
        ffn_input, gate_proj, up_proj, activated,
    ) = kept_values
    gate_proj = gate_proj.astype(jnp.float32)
    up_proj = up_proj.astype(jnp.float32)
    rows, row_length = mask.shape[:2]
    tokens = input_low.shape[0]
    incoming = incoming_low.astype(jnp.float32)
    hidden = input_low.astype(jnp.float32)
    first_inv = inv_rms(hidden)
    normed = hidden * first_inv
    second_inv = inv_rms(mid_stream)
    normed_two = mid_stream * second_inv
    act_grad = times_transposed(incoming_low, w_down)
    sigmoid_gate = jax.nn.sigmoid(gate_proj)
    gate_grad = (
        act_grad * up_proj * sigmoid_gate * (1.0 + gate_proj * (1.0 - sigmoid_gate))
    ).astype(jnp.bfloat16)
    up_grad = (act_grad * gate_proj * sigmoid_gate).astype(jnp.bfloat16)
    ffn_grad = times_transposed(gate_grad, w_gate) + times_transposed(up_grad, w_up)
    gain_two_grad = jnp.sum(ffn_grad * normed_two, axis=0)
    scaled_two = ffn_grad * gain_two
    mid_grad = incoming + second_inv * (
        scaled_two - normed_two * jnp.mean(scaled_two * normed_two, axis=-1, keepdims=True)
    )
    out_grad = mid_grad.astype(jnp.bfloat16)
    attended_grad = times_transposed(out_grad, w_out).astype(jnp.bfloat16)
    attended_grad = attended_grad.reshape(rows, row_length, KV_HEADS, GROUP, HD)
    scores = scores_of(query_rot, key_rot, mask)
    attn_probs = jnp.exp(scores - log_total)
    probs_low = attn_probs.astype(jnp.bfloat16)
    prob_grad = mixed("rtkgd,rskd->rkgts", attended_grad, value_low)
    value_grad = mixed("rkgts,rtkgd->rskd", probs_low, attended_grad)
    value_grad = value_grad.reshape(tokens, KV_HEADS * HD).astype(jnp.bfloat16)
    score_grad = (
        attn_probs * (prob_grad - jnp.sum(attn_probs * prob_grad, axis=-1, keepdims=True))
    ).astype(jnp.bfloat16)
    rot_query_grad = (
        mixed("rkgts,rskd->rtkgd", score_grad, key_rot).reshape(rows, row_length, HEADS, HD) * SCALE
    )
    rot_key_grad = mixed("rkgts,rtkgd->rskd", score_grad, query_rot) * SCALE
    cosine, sine_part = tables
    query_grad = rotate(rot_query_grad, cosine, -sine_part).reshape(tokens, HEADS * HD)
    query_grad = query_grad.astype(jnp.bfloat16)
    key_grad = rotate(rot_key_grad, cosine, -sine_part).reshape(tokens, KV_HEADS * HD)
    key_grad = key_grad.astype(jnp.bfloat16)
    attn_grad = (
        times_transposed(query_grad, w_query)
        + times_transposed(key_grad, w_key)
        + times_transposed(value_grad, w_value)
    )
    gain_one_grad = jnp.sum(attn_grad * normed, axis=0)
    scaled_one = attn_grad * gain_one
    input_grad = mid_grad + first_inv * (
        scaled_one - normed * jnp.mean(scaled_one * normed, axis=-1, keepdims=True)
    )
    grad_pieces = (query_grad, key_grad, value_grad, out_grad, gate_grad, up_grad)
    return (input_grad.astype(jnp.bfloat16), grad_pieces, gain_one_grad, gain_two_grad)


def packed_gains(first, second):
    width = first.shape[-1]
    edge = ((0, 15), (0, GAIN_LANES - width))
    return jnp.concatenate([jnp.pad(first, edge), jnp.pad(second, edge)], axis=1)


def unpacked_gains(whole, width):
    kept = whole.reshape(-1, 16, 2 * GAIN_LANES)[:, 0].astype(jnp.float32)
    return kept[:, :width].reshape(-1), kept[:, GAIN_LANES : GAIN_LANES + width].reshape(-1)


def packed_gain_sums(first, second, width):
    edge = ((0, 0), (0, GAIN_LANES - width))
    joined = jnp.concatenate(
        [jnp.pad(first.reshape(-1, width), edge), jnp.pad(second.reshape(-1, width), edge)], axis=1
    )
    spread = jnp.pad(joined[:, None, :], ((0, 0), (0, 7), (0, 0)))
    return spread.reshape(-1, 2 * GAIN_LANES)


def shards(
    tokens, cotangent, seq_lengths, w_query, w_key, w_value, w_out, w_gate, w_up, w_down, gain_attn, gain_ffn,
):
    section = lax.axis_index("pipe")
    chips = lax.axis_size("dp") // 2
    row_length = tokens.shape[0] // seq_lengths.shape[0]
    starts = row_starts(seq_lengths, row_length)
    tables = rotary_tables(starts)
    mask = attend_mask(starts)
    width = gain_attn.shape[1]
    own = [w[0] for w in (w_query, w_key, w_value, w_out, w_gate, w_up, w_down)]
    wholes = gathered(own + [packed_gains(gain_attn, gain_ffn)], chips)
    params = tuple(wholes[:7]) + unpacked_gains(wholes[7], width)

    result, kept = forward_unit(params, tokens, tables, mask)
    arrived = passed_along(result, "pipe", 1)
    result, kept = lax.cond(
        section == 1,
        lambda now: forward_unit(params, arrived, tables, mask),
        lambda now: now,
        (result, kept),
    )
    back = backward_unit(params, kept, tables, mask, cotangent)
    returned = passed_along(back[0], "pipe", -1)
    back = lax.cond(
        section == 0,
        lambda now: backward_unit(params, kept, tables, mask, returned),
        lambda now: now,
        back,
    )
    incoming = jnp.where(section == 1, cotangent, returned)
    input_grad, pieces, gain_one_grad, gain_two_grad = back
    query_grad, key_grad, value_grad, out_grad, gate_grad, up_grad = pieces
    terms = [
        across_rows(kept[1], query_grad),
        across_rows(kept[1], key_grad),
        across_rows(kept[1], value_grad),
        across_rows(kept[6], out_grad),
        across_rows(kept[8], gate_grad),
        across_rows(kept[8], up_grad),
        across_rows(kept[11], incoming),
        packed_gain_sums(gain_one_grad, gain_two_grad, width),
    ]
    sums = scattered(terms, chips)
    gains = sums[7]
    return (
        result[None],
        input_grad[None],
        *(item[None] for item in sums[:7]),
        gains[:1, :width],
        gains[:1, GAIN_LANES : GAIN_LANES + width],
    )


def solution(mesh):
    in_specs = (
        P("dp", None),
        P("dp", None),
        P("dp", None),
        P("pipe", "dp", None),
        P("pipe", "dp", None),
        P("pipe", "dp", None),
        P("pipe", "dp", None),
        P("pipe", "dp", None),
        P("pipe", "dp", None),
        P("pipe", "dp", None),
        P("pipe", "dp"),
        P("pipe", "dp"),
    )
    out_specs = (
        P("pipe", "dp", None),
        P("pipe", "dp", None),
        P("pipe", "dp", None),
        P("pipe", "dp", None),
        P("pipe", "dp", None),
        P("pipe", "dp", None),
        P("pipe", "dp", None),
        P("pipe", "dp", None),
        P("pipe", "dp", None),
        P("pipe", "dp"),
        P("pipe", "dp"),
    )
    return jax.shard_map(shards, mesh=mesh, in_specs=in_specs, out_specs=out_specs, check_vma=False)
```

time: 2170 us -> 1070 us (0.49)
  waiting for transfers between devices: 1550 us -> 138 us
  Pallas kernels: 0 us -> 523 us
  blocking collectives: 85.9 us -> 0 us
  starting transfers between devices: 64.4 us -> 5.81 us
  matrix products: 262 us -> 206 us
  local copies, waits for them, and re-layouts: 138 us -> 111 us
    reduce_scatter x7 -> x0, waiting for transfers between devices: 1010 us -> none  [the longest x1 248 us: shards(): lax.psum_scatter(terms[6], 'dp', scatter_dimension=0, tiled=True)]
    pallas_call x0 -> x2, Pallas kernels: none -> 523 us  [the longest x1 267 us: scattered(): pl.pallas_call(functools.partial(scatter_kernel, chips, count), out_shape...]
    all_gather x7 -> x0, waiting for transfers between devices: 464 us -> none  [the longest x1 101 us: shards(): lax.all_gather(w_gate, 'dp', axis=1, tiled=True)]
    another operation x34 -> x2, local copies, waits for them, and re-layouts: 69.6 us -> 4.47 us
    ppermute x6 -> x2, waiting for transfers between devices: 74.1 us -> 138 us  [passed_along(): return lax.ppermute(array, axis, pairs)]
    ppermute x6 -> x2, starting transfers between devices: 63.6 us -> 5.81 us  [passed_along(): return lax.ppermute(array, axis, pairs)]
    unnamed x1 -> x0, blocking collectives: 54.7 us -> none
    squeeze x1 -> x0, blocking collectives: 31.3 us -> none  [shards(): params = tuple((piece[0] for piece in gathered))]
  transfers between devices with their start and end apart: 20 -> 2, of which waited for: 16 -> 2; matrix products, arithmetic and copies ran while one was open for 9% -> 0% of each run, Pallas kernels for 0% -> 0%
where the time goes in v1:
time: 1070 us; the launch traced here: 1060 us
  Pallas kernels  523 us (49%)
  matrix products  206 us (19%)
  waiting for transfers between devices  138 us (13%)
  local copies, waits for them, and re-layouts  111 us (10%)
  other arithmetic  61.9 us (6%)
    pallas_call x1, Pallas kernels, scattered(): pl.pallas_call(functools.partial(scatter_kernel, chips, count), out_shape...  267 us
    pallas_call x1, Pallas kernels, gathered(): pl.pallas_call(functools.partial(gather_kernel, chips, count), out_shape=...  256 us
    ppermute x2, waiting for transfers between devices, passed_along(): return lax.ppermute(array, axis, pairs)  138 us
    dot_general x14, matrix products, times_transposed(): lax.dot_general(first_operand, second_operand, (((1,), (1,)), ((), ())),...  99.8 us
    dot_general x7, matrix products, across_rows(): lax.dot_general(first_operand, second_operand, (((0,), (0,)), ((), ())),...  45.5 us
    dot_general x7, matrix products, times(): jnp.dot(first_operand, second_operand, preferred_element_type=jnp.float32)  43.8 us
    unnamed x130, local copies, waits for them, and re-layouts  25.9 us
    reshape x4, local copies, waits for them, and re-layouts, backward_unit(): attended_grad = attended_grad.reshape(rows, row_length, KV_HEADS, GROUP, HD)  22.5 us
  transfers between devices with their start and end apart: 2, of which 2 were waited for; matrix products, arithmetic and copies ran while one was open for 0% of the time, Pallas kernels for 0%

profile of v1, /device:TPU:1, one launch (start us, length us, event | category | flops | bytes accessed | tf_op | source)
XLA Modules:
  0.0 1058.3 jit_solution(9336647131838087209)
XLA Ops:
  4.0 255.6 %gather_weights.1 = (bf16[1536,1536]{1,0:T(8,128)(2,1)}, bf16[1536,768]{1,0:T(8,128)(2,1)}, bf16[1536,768]{1,0:T(8,128)(2,1)}, bf16[1536,1536]{1,0:T(8,128)(2,1)...) custom-call(bf16[96,1536]{1,0:T(8,128)(2,1)} %bitcast.313, ...), custom_call_target="tpu_custom_call" | custom-call | tf_op jit(solution)/shard_map/gather_weights/pallas_call | solution.py:150
  267.3 3.8 fusion.121
  279.3 6.1 fusion.122
  285.4 4.1 reshape.284
  289.5 5.1 subtract_convert_fusion.5
  305.7 3.7 copy.129
  312.1 6.3 multiply_reduce_fusion.9
  320.6 5.3 fusion.123
  325.9 8.8 multiply_convert_fusion.2
  334.7 11.7 %fusion.61 = bf16[384,1536]{1,0:T(8,128)(2,1)} fusion(f32[384,1536]{1,0:T(8,128)} %get-tuple-element.701, bf16[384,4096]{1,0:T(8,128)(2,1)} %get-tuple-element.674, bf16[4096,1536]{1,0:T(8,128)(2,1)} %get-tuple-element.468), kind=kOutput, calls=%fused_computation.136 | convolution fusion | flops 4833017856 | bytes 19267584 | tf_op jit(solution)/shard_map/dot_general | solution.py:397
  346.3 4.5 collective-permute-start
  354.1 21.2 %collective-permute-done = bf16[384,1536]{1,0:T(8,128)(2,1)} collective-permute-done((bf16[384,1536]{1,0:T(8,128)(2,1)}, bf16[384,1536]{1,0:T(8,128)(2,1)}, u32[]{:S(2)}, u32[]{:S(2)}) %collective-permute-start) | collective-permute-done | bytes 1179680 | tf_op jit(solution)/shard_map/ppermute | solution.py:357
  375.3 9.1 conditional.2
  387.2 16.4 %fusion.52 = (bf16[384,4096]{1,0:T(8,128)(2,1)}, bf16[384,4096]{1,0:T(8,128)(2,1)}) fusion(bf16[384,4096]{1,0:T(8,128)(2,1)} %get-tuple-element.511, bf16[384,4096]{1,0:T(8,128)(2,1)} %get-tuple-element.512, bf16[4096,1536]{1,0:T(8,128)(2,1)} %get-tuple-element.468, bf16[384,1536]{1,0:T(8,128)(2,1)S(1)} %copy-done.26), kind=kOutput, calls=%fused_computation.104 | convolution fusion | flops 4855431168 | bytes 26345472 | tf_op jit(solution)/shard_map/dot_general | solution.py:401
  403.7 9.2 fusion.124
  412.9 11.0 %multiply_reduce_fusion.7 = (f32[384]{0:T(512)S(1)}, f32[384,1536]{1,0:T(8,128)}, f32[384,1536]{1,0:T(8,128)}) fusion(f32[1536]{0:T(1024)S(1)} %copy-done.63, f32[384,1536]{1,0:T(8,128)} %get-tuple-element.509, f32[384]{0:T(512)S(1)} %add_rsqrt_fusion.5, f32[384,1536]{1,0:T(8,128)S(1)} %fusion.124, bf16[384,4096]{1,0:T(8,128)(2,1)} %get-tuple-element.670, ...), kind=kOutput, calls=%fused_computation.149 | convolution fusion | flops 4834786816 | bytes 25175040 | tf_op jit(solution)/shard_map/dot_general | solution.py:401
  423.9 3.0 fusion.109
  428.0 3.0 convolution_convert_fusion.9
  431.0 6.2 reshape.285
  437.2 5.0 copy.132
  461.8 3.3 fusion.112
  465.1 3.2 copy.180
  468.3 3.2 copy.179
  471.5 3.7 subtract_convert_fusion.4
  477.2 4.3 convert_element_type.296
  481.6 4.9 fusion.125
  490.9 5.5 add_convert_fusion.7
  497.7 117.1 %collective-permute-done.1 = bf16[384,1536]{1,0:T(8,128)(2,1)} collective-permute-done((bf16[384,1536]{1,0:T(8,128)(2,1)}, bf16[384,1536]{1,0:T(8,128)(2,1)}, u32[]{:S(2)}, u32[]{:S(2)}) %collective-permute-start.1) | collective-permute-done | bytes 1179680 | tf_op jit(solution)/shard_map/ppermute | solution.py:357
  614.8 113.2 %conditional.3 = (bf16[384,1536]{1,0:T(8,128)(2,1)}, bf16[384,768]{1,0:T(8,128)(2,1)}, bf16[384,768]{1,0:T(8,128)(2,1)S(1)}, bf16[384,1536]{1,0:T(8,128)(2,1)}, ...) conditional(s32[]{:T(128)} %convert_element_type.287, ...), branch_computations={%region_17.18_spmd.clone, %region_18.24_spmd.clone} | conditional | flops 20747071488 | bytes 297290624 | solution.py:565
  621.6 11.5 %fusion.22 = (bf16[384,4096]{1,0:T(8,128)(2,1)S(1)}, bf16[384,4096]{1,0:T(8,128)(2,1)S(1)}) fusion(bf16[384,4096]{1,0:T(8,128)(2,1)} %get-tuple-element.548, bf16[384,4096]{1,0:T(8,128)(2,1)} %get-tuple-element.547, bf16[384,1536]{1,0:T(8,128)(2,1)} %get-tuple-element.544, bf16[4096,1536]{1,0:T(8,128)(2,1)} %get-tuple-element.546), kind=kOutput, calls=%fused_computation.44 | convolution fusion | flops 4855431168 | bytes 26345472 | tf_op jit(solution)/shard_map/cond/branch_1_fun/dot_general | solution.py:401
  633.2 10.4 fusion.119
  643.6 19.2 %multiply_reduce_fusion.2 = (f32[384]{0:T(512)S(1)}, f32[384,1536]{1,0:T(8,128)}, f32[384,1536]{1,0:T(8,128)}) fusion(f32[1536]{0:T(1024)S(1)} %mul.801, f32[384,1536]{1,0:T(8,128)} %get-tuple-element.545, f32[384]{0:T(512)S(1)} %add_rsqrt_fusion.3, f32[384,1536]{1,0:T(8,128)S(1)} %fusion.119, bf16[384,4096]{1,0:T(8,128)(2,1)S(1)} %get-tuple-element.754, ...), kind=kOutput, calls=%fused_computation.65 | convolution fusion | flops 4834786816 | bytes 25175040 | tf_op jit(solution)/shard_map/cond/branch_1_fun/dot_general | solution.py:401
  662.8 3.3 fusion.46
  667.1 3.1 convolution_convert_fusion.1
  670.2 6.4 reshape.289
  676.6 4.9 copy.109
  698.3 3.4 copy.175
  704.0 3.7 subtract_convert_fusion.2
  709.7 3.3 convert_element_type.319
  713.0 4.8 fusion.120
  721.0 6.5 add_convert_fusion.3
  734.2 2.9 convolution_convert_fusion.8.refs_1_
  739.9 4.5 convolution_convert_fusion.6.refs_0_
  744.5 9.7 convolution_convert_fusion.4.refs_4_
  754.1 9.7 convolution_convert_fusion.3.refs_5_
  763.8 4.3 convolution_convert_fusion.5.refs_3_
  768.1 11.6 %convolution_convert_fusion.2.refs_6_ = bf16[4096,1536]{1,0:T(8,128)(2,1)} fusion(bf16[384,4096]{1,0:T(8,128)(2,1)} %get-tuple-element.513, bf16[384,1536]{1,0:T(8,128)(2,1)S(1)} %copy-done.28, bf16[384,1536]{1,0:T(8,128)(2,1)} %collective-permute-done.1, pred[]{:T(512)S(6)} %eq.24), kind=kOutput, calls=%fused_computation.91 | convolution fusion | flops 4838719488 | bytes 18087936 | tf_op jit(solution)/shard_map/dot_general | solution.py:407
  779.7 267.2 %scatter_grads.1 = (f32[96,1536]{1,0:T(8,128)}, f32[96,768]{1,0:T(8,128)}, f32[96,768]{1,0:T(8,128)}, f32[96,1536]{1,0:T(8,128)}, f32[96,4096]{1,0:T(8,128)}, /*...) custom-call(bf16[1536,1536]{1,0:T(8,128)(2,1)} %convolution_convert_, ...), custom_call_target="tpu_custom_call" | custom-call | tf_op jit(solution)/shard_map/scatter_grads/pallas_call | solution.py:317
  (277 shorter events, 121.2 us)
Async XLA Ops:
  2.4 443.9 %copy-start.30 = (pred[3,128,128]{1,2,0:T(8,128)(4,1)}, pred[3,128,128]{1,2,0:T(8,128)(4,1)S(1)}, u32[]{:S(2)}) copy-start(pred[3,128,128]{1,2,0:T(8,128)(4,1)S(1)} %compare_and_fusion) | copy-start | bytes 147460
  2.8 296.3 %copy-start.51 = (f32[3,128,48]{1,2,0:T(8,128)}, f32[3,128,48]{1,2,0:T(8,128)S(1)}, u32[]{:S(2)}) copy-start(f32[3,128,48]{1,2,0:T(8,128)S(1)} %get-tuple-element.695) | copy-start | bytes 221188
  2.8 348.1 %copy-start.53 = (f32[3,128,48]{1,2,0:T(8,128)}, f32[3,128,48]{1,2,0:T(8,128)S(1)}, u32[]{:S(2)}) copy-start(f32[3,128,48]{1,2,0:T(8,128)S(1)} %get-tuple-element.693) | copy-start | bytes 221188
  2.9 286.6 %copy-start.33 = (f32[3,128,48]{2,1,0:T(8,128)}, f32[3,128,48]{2,1,0:T(8,128)S(1)}, u32[]{:S(2)}) copy-start(f32[3,128,48]{2,1,0:T(8,128)S(1)} %copy.123) | copy-start | bytes 221188
  260.6 57.8 %copy-start.62 = (f32[1536]{0:T(1024)}, f32[1536]{0:T(1024)S(1)}, u32[]{:S(2)}) copy-start(f32[1536]{0:T(1024)S(1)} %mul.740) | copy-start | bytes 18436
  260.7 4.0 copy-start.65
  261.0 6.3 copy-start.40
  312.1 8.4 slice-start
  312.1 8.4 slice-start.1
  312.1 8.4 slice-start.2
  318.4 7.4 slice-start.3
  320.5 5.3 copy-start.37
  320.5 5.3 slice-start.4
  320.6 5.3 slice-start.5
  334.7 17.0 %copy-start.47 = (bf16[3,128,8,48]{1,3,2,0:T(8,128)(2,1)S(1)}, bf16[3,128,8,48]{1,3,2,0:T(8,128)(2,1)}, u32[]{:S(2)}) copy-start(bf16[3,128,8,48]{1,3,2,0:T(8,128)(2,1)} %copy-done.46) | copy-start | bytes 884740
  346.3 6.8 copy-start.82
  346.3 29.0 %collective-permute-start = (bf16[384,1536]{1,0:T(8,128)(2,1)}, bf16[384,1536]{1,0:T(8,128)(2,1)}, u32[]{:S(2)}, u32[]{:S(2)}) collective-permute-start(bf16[384,1536]{1,0:T(8,128)(2,1)} %fusion.61), channel_id=1, source_target_pairs={{0,16},{1,17},{2,18},{3,19},{4,20},{5,21},{6,22},{7,23},{8,24},{9,... | collective-permute-start | bytes 3538952 | tf_op jit(solution)/shard_map/ppermute | solution.py:357
  387.2 36.7 %copy-start.74 = (f32[384]{0:T(512)}, f32[384]{0:T(512)S(1)}, u32[]{:S(2)}) copy-start(f32[384]{0:T(512)S(1)} %add_rsqrt_fusion.5) | copy-start | bytes 4612
  403.7 9.2 copy-start.63
  403.7 24.3 %slice-start.9 = ((s8[4718592]{0:T(1024)(128)(4,1)}), s8[4194304]{0:T(1024)(128)(4,1)S(1)}, s32[]{:S(2)}) async-start(s8[4718592]{0:T(1024)(128)(4,1)} %bitcast.328), calls=%async_computation.9 | async-start | bytes 8388608
  412.9 15.1 %slice-start.10 = ((s8[4718592]{0:T(1024)(128)(4,1)}), s8[524288]{0:T(1024)(128)(4,1)S(1)}, s32[]{:S(2)}) async-start(s8[4718592]{0:T(1024)(128)(4,1)} %bitcast.328), calls=%async_computation.10 | async-start | bytes 1048576
  442.3 4.0 copy-start.58
  481.6 4.9 copy-start.10
  481.6 4.9 copy-start.23
  490.9 5.5 copy-start.2
  496.4 118.4 %collective-permute-start.1 = (bf16[384,1536]{1,0:T(8,128)(2,1)}, bf16[384,1536]{1,0:T(8,128)(2,1)}, u32[]{:S(2)}, u32[]{:S(2)}) collective-permute-start(bf16[384,1536]{1,0:T(8,128)(2,1)} %add_convert_fusion.7), channel_id=1, source_target_pairs={{16,0},{17,1},{18,2},{19,3},{20,4},{21,5},{22,6},{23,7},{24,8},{25... | collective-permute-start | bytes 3538952 | tf_op jit(solution)/shard_map/ppermute | solution.py:357
  618.1 44.6 %copy-start.72 = (f32[384]{0:T(512)}, f32[384]{0:T(512)S(1)}, u32[]{:S(2)}) copy-start(f32[384]{0:T(512)S(1)} %add_rsqrt_fusion.3) | copy-start | bytes 4612 | tf_op jit(solution)/shard_map/cond
  619.1 14.0 %copy-start.54 = (f32[3,128,48]{1,2,0:T(8,128)}, f32[3,128,48]{1,2,0:T(8,128)S(1)}, u32[]{:S(2)}) copy-start(f32[3,128,48]{1,2,0:T(8,128)S(1)} %negate_bitcast_fusion) | copy-start | bytes 221188 | tf_op jit(solution)/shard_map/cond
  633.1 10.4 copy-start.86
  633.2 10.4 copy-start.88
  633.2 34.0 %slice-start.11 = ((s8[4718592]{0:T(1024)(128)(4,1)}), s8[524288]{0:T(1024)(128)(4,1)S(1)}, s32[]{:S(2)}) async-start(s8[4718592]{0:T(1024)(128)(4,1)} %bitcast.330), calls=%async_computation.11 | async-start | bytes 1048576 | tf_op jit(solution)/shard_map/cond
  643.6 23.6 %slice-start.12 = ((s8[4718592]{0:T(1024)(128)(4,1)}), s8[4194304]{0:T(1024)(128)(4,1)S(1)}, s32[]{:S(2)}) async-start(s8[4718592]{0:T(1024)(128)(4,1)} %bitcast.330), calls=%async_computation.12 | async-start | bytes 8388608 | tf_op jit(solution)/shard_map/cond
  698.3 20.7 %copy-start.21 = (bf16[384,768]{1,0:T(8,128)(2,1)}, bf16[384,768]{1,0:T(8,128)(2,1)S(1)}, u32[]{:S(2)}) copy-start(bf16[384,768]{1,0:T(8,128)(2,1)S(1)} %convert_element_type.324) | copy-start | bytes 1769476 | tf_op jit(solution)/shard_map/cond
  713.0 4.9 copy-start.43
  713.0 4.9 copy-start.12
  713.0 4.9 copy-start.24
  720.9 6.6 copy-start.3
  720.9 6.6 copy-start.6
  721.0 6.5 copy-start.22
  739.9 4.6 copy-start.39
  739.9 4.6 copy-start.87
  744.5 9.7 copy-start.89
  754.1 9.7 copy-start.45
  754.1 9.7 copy-start.50
  763.8 4.3 copy-start.28
  1047.0 6.8 copy-start.56
  1047.0 7.6 copy-start.36
  1052.0 3.8 copy-start.35
  (39 other events, 81.2 us)

commit v2 on v1

--- a/solution.py
+++ b/solution.py
@@ -344,17 +344,10 @@
 HEADS = 16
 KV_HEADS = 8
 HD = 96
-GROUP = HEADS // KV_HEADS
 EPSILON = 1e-05
 ROPE_BASE = 100000.0
 SCALE = 1.0 / math.sqrt(HD)
 GAIN_LANES = 128
-
-
-def passed_along(array, axis, by):
-    count = lax.axis_size(axis)
-    pairs = [(i, i + by) for i in range(count) if 0 <= i + by < count]
-    return lax.ppermute(array, axis, pairs)
 
 
 def row_starts(lengths, row_length):
@@ -364,160 +357,6 @@
     return jnp.max(reached, axis=-1)
 
 
-def rotary_tables(starts):
-    row_length = starts.shape[1]
-    half_dim = HD // 2
-    places = (jnp.arange(row_length, dtype=jnp.int32)[None] - starts).astype(jnp.float32)
-    inv_freqs = jnp.exp(jnp.arange(half_dim, dtype=jnp.float32) * (-2.0 * math.log(ROPE_BASE) / HD))
-    angles = places[:, :, None] * inv_freqs[None, None, :]
-    return (jnp.cos(angles)[:, :, None, :], jnp.sin(angles)[:, :, None, :])
-
-
-def rotate(operand, cosine, sine_part):
-    half_dim = operand.shape[-1] // 2
-    front_half, back_half = (operand[..., :half_dim], operand[..., half_dim:])
-    return jnp.concatenate(
-        [front_half * cosine - back_half * sine_part, back_half * cosine + front_half * sine_part],
-        axis=-1,
-    )
-
-
-def attend_mask(starts):
-    row_length = starts.shape[1]
-    slot_ids = jnp.arange(row_length, dtype=jnp.int32)
-    same = starts[:, None, :] == starts[:, :, None]
-    return same & (slot_ids[None, None, :] <= slot_ids[None, :, None])
-
-
-def inv_rms(operand):
-    return lax.rsqrt(jnp.mean(operand * operand, axis=-1, keepdims=True) + EPSILON)
-
-
-def times(first_operand, second_operand):
-    return jnp.dot(first_operand, second_operand, preferred_element_type=jnp.float32)
-
-
-def times_transposed(first_operand, second_operand):
-    return lax.dot_general(
-        first_operand, second_operand, (((1,), (1,)), ((), ())), preferred_element_type=jnp.float32
-    )
-
-
-def across_rows(first_operand, second_operand):
-    return lax.dot_general(
-        first_operand, second_operand, (((0,), (0,)), ((), ())), preferred_element_type=jnp.float32
-    ).astype(jnp.bfloat16)
-
-
-def mixed(spec, first_operand, second_operand):
-    return jnp.einsum(spec, first_operand, second_operand, preferred_element_type=jnp.float32)
-
-
-def scores_of(query_rot, key_rot, mask):
-    raw_scores = mixed("rtkgd,rskd->rkgts", query_rot, key_rot) * SCALE
-    return jnp.where(mask[:, None, None], raw_scores, -1e30)
-
-
-def forward_unit(params, input_low, tables, mask):
-    w_query, w_key, w_value, w_out, w_gate, w_up, w_down, gain_one, gain_two = params
-    rows, row_length = mask.shape[:2]
-    tokens = input_low.shape[0]
-    hidden = input_low.astype(jnp.float32)
-    normed = hidden * inv_rms(hidden)
-    attn_input = (normed * gain_one).astype(jnp.bfloat16)
-    cosine, sine_part = tables
-    query_proj = times(attn_input, w_query).reshape(rows, row_length, HEADS, HD)
-    key_proj = times(attn_input, w_key).reshape(rows, row_length, KV_HEADS, HD)
-    value_proj = times(attn_input, w_value).reshape(rows, row_length, KV_HEADS, HD)
-    query_rot = rotate(query_proj, cosine, sine_part).astype(jnp.bfloat16)
-    query_rot = query_rot.reshape(rows, row_length, KV_HEADS, GROUP, HD)
-    key_rot = rotate(key_proj, cosine, sine_part).astype(jnp.bfloat16)
-    value_low = value_proj.astype(jnp.bfloat16)
-    scores = scores_of(query_rot, key_rot, mask)
-    row_max = jnp.max(scores, axis=-1, keepdims=True)
-    exp_scores = jnp.exp(scores - row_max)
-    exp_total = jnp.sum(exp_scores, axis=-1, keepdims=True)
-    log_total = row_max + jnp.log(exp_total)
-    probs_low = (exp_scores / exp_total).astype(jnp.bfloat16)
-    attended = mixed("rkgts,rskd->rtkgd", probs_low, value_low)
-    attended = attended.reshape(tokens, HEADS * HD).astype(jnp.bfloat16)
-    mid_stream = hidden + times(attended, w_out)
-    normed_two = mid_stream * inv_rms(mid_stream)
-    ffn_input = (normed_two * gain_two).astype(jnp.bfloat16)
-    gate_proj = times(ffn_input, w_gate)
-    up_proj = times(ffn_input, w_up)
-    activated = (jax.nn.silu(gate_proj) * up_proj).astype(jnp.bfloat16)
-    result = mid_stream + times(activated, w_down)
-    kept_values = (
-        input_low, attn_input, query_rot, key_rot, value_low, log_total, attended, mid_stream,
-        ffn_input, gate_proj.astype(jnp.bfloat16), up_proj.astype(jnp.bfloat16), activated,
-    )
-    return (result.astype(jnp.bfloat16), kept_values)
-
-
-def backward_unit(params, kept_values, tables, mask, incoming_low):
-    w_query, w_key, w_value, w_out, w_gate, w_up, w_down, gain_one, gain_two = params
-    (
-        input_low, attn_input, query_rot, key_rot, value_low, log_total, attended, mid_stream,
-        ffn_input, gate_proj, up_proj, activated,
-    ) = kept_values
-    gate_proj = gate_proj.astype(jnp.float32)
-    up_proj = up_proj.astype(jnp.float32)
-    rows, row_length = mask.shape[:2]
-    tokens = input_low.shape[0]
-    incoming = incoming_low.astype(jnp.float32)
-    hidden = input_low.astype(jnp.float32)
-    first_inv = inv_rms(hidden)
-    normed = hidden * first_inv
-    second_inv = inv_rms(mid_stream)
-    normed_two = mid_stream * second_inv
-    act_grad = times_transposed(incoming_low, w_down)
-    sigmoid_gate = jax.nn.sigmoid(gate_proj)
-    gate_grad = (
-        act_grad * up_proj * sigmoid_gate * (1.0 + gate_proj * (1.0 - sigmoid_gate))
-    ).astype(jnp.bfloat16)
-    up_grad = (act_grad * gate_proj * sigmoid_gate).astype(jnp.bfloat16)
-    ffn_grad = times_transposed(gate_grad, w_gate) + times_transposed(up_grad, w_up)
-    gain_two_grad = jnp.sum(ffn_grad * normed_two, axis=0)
-    scaled_two = ffn_grad * gain_two
-    mid_grad = incoming + second_inv * (
-        scaled_two - normed_two * jnp.mean(scaled_two * normed_two, axis=-1, keepdims=True)
-    )
-    out_grad = mid_grad.astype(jnp.bfloat16)
-    attended_grad = times_transposed(out_grad, w_out).astype(jnp.bfloat16)
-    attended_grad = attended_grad.reshape(rows, row_length, KV_HEADS, GROUP, HD)
-    scores = scores_of(query_rot, key_rot, mask)
-    attn_probs = jnp.exp(scores - log_total)
-    probs_low = attn_probs.astype(jnp.bfloat16)
-    prob_grad = mixed("rtkgd,rskd->rkgts", attended_grad, value_low)
-    value_grad = mixed("rkgts,rtkgd->rskd", probs_low, attended_grad)
-    value_grad = value_grad.reshape(tokens, KV_HEADS * HD).astype(jnp.bfloat16)
-    score_grad = (
-        attn_probs * (prob_grad - jnp.sum(attn_probs * prob_grad, axis=-1, keepdims=True))
-    ).astype(jnp.bfloat16)
-    rot_query_grad = (
-        mixed("rkgts,rskd->rtkgd", score_grad, key_rot).reshape(rows, row_length, HEADS, HD) * SCALE
-    )
-    rot_key_grad = mixed("rkgts,rtkgd->rskd", score_grad, query_rot) * SCALE
-    cosine, sine_part = tables
-    query_grad = rotate(rot_query_grad, cosine, -sine_part).reshape(tokens, HEADS * HD)
-    query_grad = query_grad.astype(jnp.bfloat16)
-    key_grad = rotate(rot_key_grad, cosine, -sine_part).reshape(tokens, KV_HEADS * HD)
-    key_grad = key_grad.astype(jnp.bfloat16)
-    attn_grad = (
-        times_transposed(query_grad, w_query)
-        + times_transposed(key_grad, w_key)
-        + times_transposed(value_grad, w_value)
-    )
-    gain_one_grad = jnp.sum(attn_grad * normed, axis=0)
-    scaled_one = attn_grad * gain_one
-    input_grad = mid_grad + first_inv * (
-        scaled_one - normed * jnp.mean(scaled_one * normed, axis=-1, keepdims=True)
-    )
-    grad_pieces = (query_grad, key_grad, value_grad, out_grad, gate_grad, up_grad)
-    return (input_grad.astype(jnp.bfloat16), grad_pieces, gain_one_grad, gain_two_grad)
-
-
 def packed_gains(first, second):
     width = first.shape[-1]
     edge = ((0, 15), (0, GAIN_LANES - width))
@@ -526,7 +365,7 @@
 
 def unpacked_gains(whole, width):
     kept = whole.reshape(-1, 16, 2 * GAIN_LANES)[:, 0].astype(jnp.float32)
-    return kept[:, :width].reshape(-1), kept[:, GAIN_LANES : GAIN_LANES + width].reshape(-1)
+    return kept[:, :width].reshape(1, -1), kept[:, GAIN_LANES : GAIN_LANES + width].reshape(1, -1)
 
 
 def packed_gain_sums(first, second, width):
@@ -538,50 +377,624 @@
     return spread.reshape(-1, 2 * GAIN_LANES)
 
 
+def spread_heads(tile, lane):
+    first, second, third = tile[:, :128], tile[:, 128:256], tile[:, 256:384]
+    return (
+        first,
+        jnp.where(lane < 32, pltpu.roll(first, 32, 1), pltpu.roll(second, 32, 1)),
+        jnp.where(lane < 64, pltpu.roll(second, 64, 1), pltpu.roll(third, 64, 1)),
+        pltpu.roll(third, 96, 1),
+    )
+
+
+def joined_heads(heads, lane):
+    one, two, three = pltpu.roll(heads[1], 96, 1), pltpu.roll(heads[2], 64, 1), pltpu.roll(heads[3], 32, 1)
+    return (
+        jnp.where(lane < 96, heads[0], one),
+        jnp.where(lane < 64, one, two),
+        jnp.where(lane < 32, two, three),
+    )
+
+
+def turned(head, cosine, fore, aft):
+    return head * cosine + pltpu.roll(head, 80, 1) * fore + pltpu.roll(head, 48, 1) * aft
+
+
+def streamed(count, depth, copies, use):
+    def body(j, carry):
+        @pl.when(j + depth - 1 < count)
+        def _():
+            for copy in copies(j + depth - 1, (j + depth - 1) % depth):
+                copy.start()
+
+        for copy in copies(j, j % depth):
+            copy.wait()
+        use(j, j % depth)
+        return carry
+
+    lax.fori_loop(0, count, body, 0)
+
+
+def lead(count, depth, copies):
+    for j in range(min(depth - 1, count)):
+        for copy in copies(j, j % depth):
+            copy.start()
+
+
+def normal_rows(source, target, gain, rows):
+    band_rows = 64
+
+    def body(i, carry):
+        band = pl.ds(pl.multiple_of(i * band_rows, band_rows), band_rows)
+        value = source[band, :].astype(jnp.float32)
+        scale = lax.rsqrt(jnp.mean(value * value, axis=-1, keepdims=True) + EPSILON)
+        target[band, :] = ((value * scale) * gain[...]).astype(jnp.bfloat16)
+        return carry
+
+    lax.fori_loop(0, rows // band_rows, body, 0)
+
+
+def head_lane():
+    return lax.broadcasted_iota(jnp.int32, (MB, 128), 1)
+
+
+MB = 128
+FWD_KEPT = ("attn_input", "queries", "keys", "values", "probs", "attended", "mid", "ffn_input", "gate", "up", "activated")
+
+
+def forward_kernel(rows, *refs):
+    (tokens, seg_column, seg_row, cosine, fore, aft, gain_one, gain_two,
+     w_query, w_key, w_value, w_out, w_gate, w_up, w_down,
+     out_ref, source_ref, attn_input_o, queries_o, keys_o, values_o, probs_o, attended_o, mid_o, ffn_input_o, gate_o, up_o, activated_o,
+     source, result, attn_input, queries, keys, values, probs, attended, mid, ffn_input, gate, up, activated,
+     square, pair_slot, tall,
+     square_sem, pair_sem, tall_sem, keep_sem, load_sem, send_sem, recv_sem) = refs
+    section = lax.axis_index("pipe")
+    width = tokens.shape[1]
+    inner = w_gate.shape[1]
+    kv_width = w_key.shape[1]
+    micro = rows // MB
+    barrier = pltpu.get_barrier_semaphore()
+    pl.semaphore_signal(barrier, inc=1, device_id={"pipe": 1 - section}, device_id_type=MESH)
+    pl.semaphore_wait(barrier, 1)
+
+    def pass_on(part):
+        band = pl.ds(part * MB, MB)
+        return pltpu.make_async_remote_copy(
+            src_ref=result.at[band, :], dst_ref=source.at[band, :],
+            send_sem=send_sem.at[part], recv_sem=recv_sem.at[part],
+            device_id={"pipe": 1 - section}, device_id_type=MESH,
+        )
+
+    step = 768
+    per_query = width // step
+    per_kv = kv_width // step
+
+    def qkv_copies(j):
+        if j < per_query:
+            weight, at = w_query, j
+        elif j < per_query + per_kv:
+            weight, at = w_key, j - per_query
+        else:
+            weight, at = w_value, j - per_query - per_kv
+        return pltpu.make_async_copy(
+            weight.at[:, pl.ds(at * step, step)], square.at[j % 4], square_sem.at[j % 4]
+        )
+
+    def out_copy(j):
+        return pltpu.make_async_copy(
+            w_out.at[:, pl.ds(j * step, step)], square.at[j % 4], square_sem.at[j % 4]
+        )
+
+    wide = 1024
+
+    def ffn_copies(j, slot):
+        column = pl.ds(pl.multiple_of(j * wide, wide), wide)
+        return (
+            pltpu.make_async_copy(w_gate.at[:, column], pair_slot.at[slot, 0], pair_sem.at[slot, 0]),
+            pltpu.make_async_copy(w_up.at[:, column], pair_slot.at[slot, 1], pair_sem.at[slot, 1]),
+        )
+
+    narrow = 512
+
+    def down_copies(j, slot):
+        column = pl.ds(pl.multiple_of(j * narrow, narrow), narrow)
+        return (pltpu.make_async_copy(w_down.at[:, column], tall.at[slot], tall_sem.at[slot]),)
+
+    count_qkv = per_query + 2 * per_kv
+    for j in range(4):
+        qkv_copies(j).start()
+    lead(inner // wide, 2, ffn_copies)
+    lead(width // narrow, 2, down_copies)
+
+    @pl.when(section == 0)
+    def _():
+        load = pltpu.make_async_copy(tokens, source, load_sem)
+        load.start()
+        load.wait()
+
+    @pl.when(section == 1)
+    def _():
+        for part in range(micro):
+            pass_on(part).wait_recv()
+
+    kept = []
+
+    def keep(index, here, there):
+        copy = pltpu.make_async_copy(here, there, keep_sem.at[index])
+        copy.start()
+        kept.append(copy)
+
+    keep(12, source, source_ref)
+    normal_rows(source, attn_input, gain_one, rows)
+    keep(0, attn_input, attn_input_o)
+    lane = lax.broadcasted_iota(jnp.int32, (rows, 128), 1)
+
+    def project(j):
+        qkv_copies(j).wait()
+        value = jnp.dot(attn_input[...], square[j % 4], preferred_element_type=jnp.float32)
+        if j + 4 < count_qkv:
+            qkv_copies(j + 4).start()
+        elif j + 4 - count_qkv < width // step:
+            pass
+        return value
+
+    for j in range(count_qkv):
+        value = project(j)
+        for part in range(2):
+            heads = spread_heads(value[:, part * 384 : part * 384 + 384], lane)
+            for k in range(4):
+                if j < per_query + per_kv:
+                    low = turned(heads[k], cosine[...], fore[...], aft[...]).astype(jnp.bfloat16)
+                else:
+                    low = jnp.where(lane < HD, heads[k], 0.0).astype(jnp.bfloat16)
+                if j < per_query:
+                    at, target = j * 8 + part * 4 + k, queries
+                elif j < per_query + per_kv:
+                    at, target = (j - per_query) * 8 + part * 4 + k, keys
+                else:
+                    at, target = (j - per_query - per_kv) * 8 + part * 4 + k, values
+                target[:, pl.ds(at * 128, 128)] = low
+    for j in range(width // step):
+        out_copy(j).start()
+    keep(1, queries, queries_o)
+    keep(2, keys, keys_o)
+    keep(3, values, values_o)
+
+    def attend(at, carry):
+        row = at // 2
+        quad = at % 2
+        band = pl.ds(pl.multiple_of(row * MB, MB), MB)
+        slot_i = lax.broadcasted_iota(jnp.int32, (2 * MB, MB), 0)
+        slot_i = jnp.where(slot_i >= MB, slot_i - MB, slot_i)
+        slot_j = lax.broadcasted_iota(jnp.int32, (2 * MB, MB), 1)
+        column = seg_column[band, :]
+        same = jnp.concatenate([column, column], axis=0) == seg_row[pl.ds(row, 1), :]
+        mask = same & (slot_j <= slot_i)
+        small = head_lane()
+        outs = []
+        for k in range(4):
+            kv = pl.ds(pl.multiple_of((quad * 4 + k) * 128, 128), 128)
+            pair = quad * 8 + 2 * k
+            query = jnp.concatenate(
+                [
+                    queries[band, pl.ds(pl.multiple_of(pair * 128, 128), 128)],
+                    queries[band, pl.ds(pl.multiple_of((pair + 1) * 128, 128), 128)],
+                ],
+                axis=0,
+            )
+            scores = lax.dot_general(
+                query, keys[band, kv], (((1,), (1,)), ((), ())), preferred_element_type=jnp.float32
+            ) * SCALE
+            scores = jnp.where(mask, scores, -1e30)
+            high = jnp.max(scores, axis=-1, keepdims=True)
+            grown = jnp.exp(scores - high)
+            low = (grown / jnp.sum(grown, axis=-1, keepdims=True)).astype(jnp.bfloat16)
+            place = pl.ds(pl.multiple_of((at * 4 + k) * 2 * MB, 2 * MB), 2 * MB)
+            probs[place, :] = low
+            out = jnp.dot(low, values[band, kv], preferred_element_type=jnp.float32)
+            outs += [out[:MB], out[MB:]]
+        for part in range(2):
+            for c, piece in enumerate(joined_heads(outs[part * 4 : part * 4 + 4], small)):
+                column = pl.ds(pl.multiple_of(quad * 768 + part * 384 + c * 128, 128), 128)
+                attended[band, column] = piece.astype(jnp.bfloat16)
+        return carry
+
+    lax.fori_loop(0, 2 * micro, attend, 0)
+    keep(4, probs, probs_o)
+    keep(5, attended, attended_o)
+    for j in range(width // step):
+        out_copy(j).wait()
+        column = pl.ds(j * step, step)
+        mid[:, column] = source[:, column].astype(jnp.float32) + jnp.dot(
+            attended[...], square[j % 4], preferred_element_type=jnp.float32
+        )
+    keep(6, mid, mid_o)
+    normal_rows(mid, ffn_input, gain_two, rows)
+    keep(7, ffn_input, ffn_input_o)
+
+    def expand(j, slot):
+        column = pl.ds(pl.multiple_of(j * wide, wide), wide)
+        gate_part = jnp.dot(ffn_input[...], pair_slot[slot, 0], preferred_element_type=jnp.float32)
+        up_part = jnp.dot(ffn_input[...], pair_slot[slot, 1], preferred_element_type=jnp.float32)
+        gate[:, column] = gate_part.astype(jnp.bfloat16)
+        up[:, column] = up_part.astype(jnp.bfloat16)
+        activated[:, column] = (gate_part / (1.0 + jnp.exp(-gate_part)) * up_part).astype(jnp.bfloat16)
+
+    streamed(inner // wide, 2, ffn_copies, expand)
+    keep(8, gate, gate_o)
+    keep(9, up, up_o)
+    keep(10, activated, activated_o)
+
+    def contract(j, slot):
+        column = pl.ds(pl.multiple_of(j * narrow, narrow), narrow)
+        value = mid[:, column] + jnp.dot(activated[...], tall[slot], preferred_element_type=jnp.float32)
+        result[:, column] = value.astype(jnp.bfloat16)
+
+    streamed(width // narrow, 2, down_copies, contract)
+    keep(11, result, out_ref)
+
+    @pl.when(section == 0)
+    def _():
+        for part in range(micro):
+            pass_on(part).start()
+        for part in range(micro):
+            pass_on(part).wait_send()
+
+    for copy in kept:
+        copy.wait()
+
+
+def forward_call(tokens, starts, tables, gain_one, gain_two, weights):
+    rows, width = tokens.shape
+    micro = rows // MB
+    inner = weights[4].shape[1]
+    kv_width = weights[1].shape[1]
+    low, full = jnp.bfloat16, jnp.float32
+    S = jax.ShapeDtypeStruct
+    kept = [
+        S((rows, width), low), S((rows, HEADS * 128), low), S((rows, KV_HEADS * 128), low), S((rows, KV_HEADS * 128), low),
+        S((micro * HEADS * MB, MB), low), S((rows, width), low), S((rows, width), full), S((rows, width), low),
+        S((rows, inner), low), S((rows, inner), low), S((rows, inner), low),
+    ]
+    anywhere = pl.BlockSpec(memory_space=pl.ANY)
+    local = pl.BlockSpec(memory_space=pltpu.VMEM)
+    square = 1536 // 2
+    outs = pl.pallas_call(
+        functools.partial(forward_kernel, rows),
+        out_shape=[S((rows, width), low), S((rows, width), low)] + kept,
+        in_specs=[anywhere] + [local] * 7 + [anywhere] * 7,
+        out_specs=[anywhere] * (2 + len(kept)),
+        scratch_shapes=[pltpu.VMEM((rows, width), low), pltpu.VMEM((rows, width), low)]
+        + [pltpu.VMEM(k.shape, k.dtype) for k in kept]
+        + [
+            pltpu.VMEM((4, width, square), low),
+            pltpu.VMEM((2, 2, width, 1024), low),
+            pltpu.VMEM((2, inner, 512), low),
+            pltpu.SemaphoreType.DMA((4,)),
+            pltpu.SemaphoreType.DMA((2, 2)),
+            pltpu.SemaphoreType.DMA((2,)),
+            pltpu.SemaphoreType.DMA((13,)),
+            pltpu.SemaphoreType.DMA,
+            pltpu.SemaphoreType.DMA((micro,)),
+            pltpu.SemaphoreType.DMA((micro,)),
+        ],
+        compiler_params=pltpu.CompilerParams(collective_id=2, has_side_effects=True, vmem_limit_bytes=63 << 20),
+        name="forward_layers",
+    )(tokens, starts.reshape(rows, 1), starts, *tables, gain_one, gain_two, *weights)
+    return outs[0], outs[1], outs[2:]
+
+
+def padded_tables(starts):
+    places = (jnp.arange(starts.shape[1], dtype=jnp.int32)[None] - starts).astype(jnp.float32).reshape(-1, 1)
+    lanes = jnp.arange(128, dtype=jnp.int32)
+    half = HD // 2
+    inv_freqs = jnp.exp((lanes % half).astype(jnp.float32) * (-2.0 * math.log(ROPE_BASE) / HD))
+    angles = places * inv_freqs[None]
+    cosine, sine = jnp.cos(angles), jnp.sin(angles)
+    return (
+        jnp.where(lanes < HD, cosine, 0.0),
+        jnp.where(lanes < half, -sine, 0.0),
+        jnp.where((lanes >= half) & (lanes < HD), sine, 0.0),
+    )
+
+
+def dot_nt(first, second):
+    return lax.dot_general(first, second, (((1,), (1,)), ((), ())), preferred_element_type=jnp.float32)
+
+
+def dot_tn(first, second):
+    return lax.dot_general(first, second, (((0,), (0,)), ((), ())), preferred_element_type=jnp.float32)
+
+
+def norm_back(grad, stream, gain, upper, target, low_target, gain_sum, rows):
+    band_rows = 32
+    gain_sum[...] = jnp.zeros_like(gain_sum)
+
+    def body(i, carry):
+        band = pl.ds(pl.multiple_of(i * band_rows, band_rows), band_rows)
+        value = stream[band, :].astype(jnp.float32)
+        scale = lax.rsqrt(jnp.mean(value * value, axis=-1, keepdims=True) + EPSILON)
+        normed = value * scale
+        term = grad[band, :] * normed
+        gain_sum[...] += term.reshape(band_rows // 8, 8, term.shape[1]).sum(axis=0)
+        inner_mean = jnp.mean(term * gain[...], axis=-1, keepdims=True)
+        out = upper[band, :].astype(jnp.float32) + scale * (grad[band, :] * gain[...] - normed * inner_mean)
+        if target is not None:
+            target[band, :] = out
+        low_target[band, :] = out.astype(jnp.bfloat16)
+        return carry
+
+    lax.fori_loop(0, rows // band_rows, body, 0)
+
+
+def backward_kernel(rows, *refs):
+    (cotangent, cosine, fore, aft, gain_one, gain_two,
+     w_query, w_key, w_value, w_out, w_gate, w_up, w_down,
+     source_i, attn_input_i, queries_i, keys_i, values_i, probs_i, attended_i, mid_i, ffn_input_i, gate_i, up_i, activated_i,
+     out_ref, gain_one_o, gain_two_o, g_query, g_key, g_value, g_out, g_gate, g_up, g_down,
+     incoming, passed, activated, ffn_input, attn_input, attended, source, mid, probs, queries, keys, values,
+     gate_grad, up_grad, stream_grad, out_grad, heads_grad, query_grad, key_grad, value_grad,
+     gate_slot, flat, kv_slot, pair_slot, flat_stage, wide_stage,
+     gate_sem, flat_sem, kv_sem, pair_sem, flat_out, wide_out, load_sem, send_sem, recv_sem) = refs
+    section = lax.axis_index("pipe")
+    width = cotangent.shape[1]
+    inner = w_gate.shape[1]
+    kv_width = w_key.shape[1]
+    micro = rows // MB
+    barrier = pltpu.get_barrier_semaphore()
+    pl.semaphore_signal(barrier, inc=1, device_id={"pipe": 1 - section}, device_id_type=MESH)
+    pl.semaphore_wait(barrier, 1)
+
+    def pass_on(part):
+        band = pl.ds(part * MB, MB)
+        return pltpu.make_async_remote_copy(
+            src_ref=passed.at[band, :], dst_ref=incoming.at[band, :],
+            send_sem=send_sem.at[part], recv_sem=recv_sem.at[part],
+            device_id={"pipe": 1 - section}, device_id_type=MESH,
+        )
+
+    def loading(index, there, here):
+        copy = pltpu.make_async_copy(there, here, load_sem.at[index])
+        copy.start()
+        return copy
+
+    act_load = loading(0, activated_i, activated)
+    mid_load = loading(1, mid_i, mid)
+    rest_loads = [
+        loading(2 + i, there, here)
+        for i, (there, here) in enumerate(
+            ((probs_i, probs), (queries_i, queries), (keys_i, keys), (values_i, values),
+             (source_i, source), (ffn_input_i, ffn_input), (attn_input_i, attn_input), (attended_i, attended))
+        )
+    ]
+    step = 512
+
+    def flat_copy(weight, j, slot):
+        return pltpu.make_async_copy(
+            weight.at[pl.ds(pl.multiple_of(j * step, step), step), :], flat.at[slot], flat_sem.at[slot]
+        )
+
+    def down_copies(j, slot):
+        column = pl.ds(pl.multiple_of(j * step, step), step)
+        return (
+            flat_copy(w_down, j, slot),
+            pltpu.make_async_copy(gate_i.at[:, column], gate_slot.at[slot, 0], gate_sem.at[slot, 0]),
+            pltpu.make_async_copy(up_i.at[:, column], gate_slot.at[slot, 1], gate_sem.at[slot, 1]),
+        )
+
+    def out_copies(j, slot):
+        return (flat_copy(w_out, j, slot),)
+
+    def qkv_copies(j, slot):
+        band = pl.ds(pl.multiple_of(j * step, step), step)
+        return (
+            flat_copy(w_query, j, slot),
+            pltpu.make_async_copy(w_key.at[band, :], kv_slot.at[slot, 0], kv_sem.at[slot, 0]),
+            pltpu.make_async_copy(w_value.at[band, :], kv_slot.at[slot, 1], kv_sem.at[slot, 1]),
+        )
+
+    short = 256
+
+    def ffn_copies(j, slot):
+        band = pl.ds(pl.multiple_of(j * short, short), short)
+        return (
+            pltpu.make_async_copy(w_gate.at[band, :], pair_slot.at[slot, 0], pair_sem.at[slot, 0]),
+            pltpu.make_async_copy(w_up.at[band, :], pair_slot.at[slot, 1], pair_sem.at[slot, 1]),
+        )
+
+    lead(inner // step, 3, down_copies)
+    lead(width // short, 2, ffn_copies)
+
+    @pl.when(section == 1)
+    def _():
+        load = loading(10, cotangent, incoming)
+        load.wait()
+
+    @pl.when(section == 0)
+    def _():
+        for part in range(micro):
+            pass_on(part).wait_recv()
+
+    def staged(left, left_step, right, stage, sems, targets):
+        count = left.shape[1] // left_step
+        columns = right.shape[1]
+
+        def put(j, slot):
+            band = pl.ds(pl.multiple_of(j * left_step, left_step), left_step)
+            return pltpu.make_async_copy(
+                stage.at[slot, :, pl.ds(0, columns)], targets.at[band, :], sems.at[slot]
+            )
+
+        def body(j, carry):
+            @pl.when(j >= 2)
+            def _():
+                put(j - 2, j % 2).wait()
+
+            column = pl.ds(pl.multiple_of(j * left_step, left_step), left_step)
+            stage[j % 2, :, pl.ds(0, columns)] = dot_tn(left[:, column], right[...]).astype(jnp.bfloat16)
+            put(j, j % 2).start()
+            return carry
+
+        lax.fori_loop(0, count, body, 0)
+        for j in range(max(0, count - 2), count):
+            put(j, j % 2).wait()
+
+    def contract_back(j, slot):
+        column = pl.ds(pl.multiple_of(j * step, step), step)
+        act_grad = dot_nt(incoming[...], flat[slot])
+        gate = gate_slot[slot, 0].astype(jnp.float32)
+        up = gate_slot[slot, 1].astype(jnp.float32)
+        sigmoid = 1.0 / (1.0 + jnp.exp(-gate))
+        gate_grad[:, column] = (act_grad * up * sigmoid * (1.0 + gate * (1.0 - sigmoid))).astype(jnp.bfloat16)
+        up_grad[:, column] = (act_grad * gate * sigmoid).astype(jnp.bfloat16)
+
+    streamed(inner // step, 3, down_copies, contract_back)
+    lead(width // step, 3, out_copies)
+
+    def expand_back(j, slot):
+        column = pl.ds(pl.multiple_of(j * short, short), short)
+        stream_grad[:, column] = dot_nt(gate_grad[...], pair_slot[slot, 0]) + dot_nt(up_grad[...], pair_slot[slot, 1])
+
+    streamed(width // short, 2, ffn_copies, expand_back)
+    mid_load.wait()
+    norm_back(stream_grad, mid, gain_two, incoming, mid, out_grad, gain_two_o, rows)
+    lane = lax.broadcasted_iota(jnp.int32, (rows, 128), 1)
+
+    def attended_back(j, slot):
+        column = pl.ds(pl.multiple_of(j * step, step), step)
+        stream_grad[:, column] = dot_nt(out_grad[...], flat[slot])
+
+    streamed(width // step, 3, out_copies, attended_back)
+    lead(width // step, 3, qkv_copies)
+    for part in range(width // 384):
+        tile = stream_grad[:, pl.ds(part * 384, 384)]
+        for k, head in enumerate(spread_heads(tile, lane)):
+            heads_grad[:, pl.ds((part * 4 + k) * 128, 128)] = jnp.where(lane < HD, head, 0.0).astype(jnp.bfloat16)
+    for copy in rest_loads:
+        copy.wait()
+
+    def attend_back(at, carry):
+        row = at // 2
+        quad = at % 2
+        band = pl.ds(pl.multiple_of(row * MB, MB), MB)
+        small = head_lane()
+        table = (cosine[band, :], fore[band, :], aft[band, :])
+
+        def unturned(head):
+            return head * table[0] - pltpu.roll(head, 80, 1) * table[1] - pltpu.roll(head, 48, 1) * table[2]
+
+        query_parts, key_parts, value_parts = [], [], []
+        for k in range(4):
+            kv = pl.ds(pl.multiple_of((quad * 4 + k) * 128, 128), 128)
+            pair = quad * 8 + 2 * k
+            first = pl.ds(pl.multiple_of(pair * 128, 128), 128)
+            second = pl.ds(pl.multiple_of((pair + 1) * 128, 128), 128)
+            query = jnp.concatenate([queries[band, first], queries[band, second]], axis=0)
+            out = jnp.concatenate([heads_grad[band, first], heads_grad[band, second]], axis=0)
+            low = probs[pl.ds(pl.multiple_of((at * 4 + k) * 2 * MB, 2 * MB), 2 * MB), :]
+            prob_grad = dot_nt(out, values[band, kv])
+            value_parts.append(dot_tn(low, out))
+            full = low.astype(jnp.float32)
+            score = full * (prob_grad - jnp.sum(full * prob_grad, axis=-1, keepdims=True))
+            score = score.astype(jnp.bfloat16)
+            back = jnp.dot(score, keys[band, kv], preferred_element_type=jnp.float32) * SCALE
+            query_parts += [unturned(back[:MB]), unturned(back[MB:])]
+            key_parts.append(unturned(dot_tn(score, query) * SCALE))
+        for part in range(2):
+            for c, piece in enumerate(joined_heads(query_parts[part * 4 : part * 4 + 4], small)):
+                column = pl.ds(pl.multiple_of(quad * 768 + part * 384 + c * 128, 128), 128)
+                query_grad[band, column] = piece.astype(jnp.bfloat16)
+        for parts, target in ((key_parts, key_grad), (value_parts, value_grad)):
+            for c, piece in enumerate(joined_heads(parts, small)):
+                column = pl.ds(pl.multiple_of(quad * 384 + c * 128, 128), 128)
+                target[band, column] = piece.astype(jnp.bfloat16)
+        return carry
+
+    lax.fori_loop(0, 2 * micro, attend_back, 0)
+
+    def project_back(j, slot):
+        column = pl.ds(pl.multiple_of(j * step, step), step)
+        stream_grad[:, column] = (
+            dot_nt(query_grad[...], flat[slot])
+            + dot_nt(key_grad[...], kv_slot[slot, 0])
+            + dot_nt(value_grad[...], kv_slot[slot, 1])
+        )
+
+    streamed(width // step, 3, qkv_copies, project_back)
+    norm_back(stream_grad, source, gain_one, mid, None, passed, gain_one_o, rows)
+
+    @pl.when(section == 1)
+    def _():
+        for part in range(micro):
+            pass_on(part).start()
+
+    keep = loading(11, passed, out_ref)
+    act_load.wait()
+    staged(activated, step, incoming, flat_stage, flat_out, g_down)
+    staged(ffn_input, short, gate_grad, wide_stage, wide_out, g_gate)
+    staged(ffn_input, short, up_grad, wide_stage, wide_out, g_up)
+    staged(attended, step, out_grad, flat_stage, flat_out, g_out)
+    staged(attn_input, step, query_grad, flat_stage, flat_out, g_query)
+    staged(attn_input, step, key_grad, flat_stage, flat_out, g_key)
+    staged(attn_input, step, value_grad, flat_stage, flat_out, g_value)
+    keep.wait()
+
+    @pl.when(section == 1)
+    def _():
+        for part in range(micro):
+            pass_on(part).wait_send()
+
+
+def backward_call(cotangent, tables, gain_one, gain_two, weights, source, kept):
+    rows, width = cotangent.shape
+    micro = rows // MB
+    inner = weights[4].shape[1]
+    kv_width = weights[1].shape[1]
+    low, full = jnp.bfloat16, jnp.float32
+    S = jax.ShapeDtypeStruct
+    anywhere = pl.BlockSpec(memory_space=pl.ANY)
+    local = pl.BlockSpec(memory_space=pltpu.VMEM)
+    V = pltpu.VMEM
+    D = pltpu.SemaphoreType.DMA
+    outs = pl.pallas_call(
+        functools.partial(backward_kernel, rows),
+        out_shape=[S((rows, width), low), S((8, width), full), S((8, width), full)]
+        + [S(w.shape, low) for w in weights],
+        in_specs=[anywhere] + [local] * 5 + [anywhere] * (8 + len(kept)),
+        out_specs=[anywhere, local, local] + [anywhere] * 7,
+        scratch_shapes=[
+            V((rows, width), low), V((rows, width), low),
+            V((rows, inner), low), V((rows, width), low), V((rows, width), low), V((rows, width), low), V((rows, width), low),
+            V((rows, width), full), V(kept[4].shape, low), V(kept[1].shape, low), V(kept[2].shape, low), V(kept[3].shape, low),
+            V((rows, inner), low), V((rows, inner), low), V((rows, width), full), V((rows, width), low), V((rows, HEADS * 128), low),
+            V((rows, width), low), V((rows, kv_width), low), V((rows, kv_width), low),
+            V((3, 2, rows, 512), low), V((3, 512, width), low), V((3, 2, 512, kv_width), low), V((2, 2, 256, inner), low),
+            V((2, 512, width), low), V((2, 256, inner), low),
+            D((3, 2)), D((3,)), D((3, 2)), D((2, 2)), D((2,)), D((2,)), D((12,)), D((micro,)), D((micro,)),
+        ],
+        compiler_params=pltpu.CompilerParams(collective_id=3, has_side_effects=True, vmem_limit_bytes=63 << 20),
+        name="backward_layers",
+    )(cotangent, *tables, gain_one, gain_two, *weights, source, *kept)
+    return outs[0], outs[1].sum(axis=0), outs[2].sum(axis=0), list(outs[3:])
+
+
 def shards(
     tokens, cotangent, seq_lengths, w_query, w_key, w_value, w_out, w_gate, w_up, w_down, gain_attn, gain_ffn,
 ):
-    section = lax.axis_index("pipe")
     chips = lax.axis_size("dp") // 2
-    row_length = tokens.shape[0] // seq_lengths.shape[0]
-    starts = row_starts(seq_lengths, row_length)
-    tables = rotary_tables(starts)
-    mask = attend_mask(starts)
+    starts = row_starts(seq_lengths, tokens.shape[0] // seq_lengths.shape[0])
+    tables = padded_tables(starts)
     width = gain_attn.shape[1]
     own = [w[0] for w in (w_query, w_key, w_value, w_out, w_gate, w_up, w_down)]
     wholes = gathered(own + [packed_gains(gain_attn, gain_ffn)], chips)
-    params = tuple(wholes[:7]) + unpacked_gains(wholes[7], width)
-
-    result, kept = forward_unit(params, tokens, tables, mask)
-    arrived = passed_along(result, "pipe", 1)
-    result, kept = lax.cond(
-        section == 1,
-        lambda now: forward_unit(params, arrived, tables, mask),
-        lambda now: now,
-        (result, kept),
+    weights = wholes[:7]
+    gain_one, gain_two = unpacked_gains(wholes[7], width)
+    result, source, kept = forward_call(tokens, starts, tables, gain_one, gain_two, weights)
+    input_grad, gain_one_grad, gain_two_grad, terms = backward_call(
+        cotangent, tables, gain_one, gain_two, weights, source, kept
     )
-    back = backward_unit(params, kept, tables, mask, cotangent)
-    returned = passed_along(back[0], "pipe", -1)
-    back = lax.cond(
-        section == 0,
-        lambda now: backward_unit(params, kept, tables, mask, returned),
-        lambda now: now,
-        back,
-    )
-    incoming = jnp.where(section == 1, cotangent, returned)
-    input_grad, pieces, gain_one_grad, gain_two_grad = back
-    query_grad, key_grad, value_grad, out_grad, gate_grad, up_grad = pieces
-    terms = [
-        across_rows(kept[1], query_grad),
-        across_rows(kept[1], key_grad),
-        across_rows(kept[1], value_grad),
-        across_rows(kept[6], out_grad),
-        across_rows(kept[8], gate_grad),
-        across_rows(kept[8], up_grad),
-        across_rows(kept[11], incoming),
-        packed_gain_sums(gain_one_grad, gain_two_grad, width),
-    ]
-    sums = scattered(terms, chips)
+    sums = scattered(terms + [packed_gain_sums(gain_one_grad, gain_two_grad, width)], chips)
     gains = sums[7]
     return (
         result[None],

time: 1070 us -> 822 us (0.77); the launches traced: 1060 us -> 821 us
  Pallas kernels: 523 us -> 800 us
  matrix products: 206 us -> 0 us
  waiting for transfers between devices: 138 us -> 0 us
  local copies, waits for them, and re-layouts: 111 us -> 14.5 us
  other arithmetic: 61.9 us -> 5.5 us
    pallas_call x0 -> x2, Pallas kernels: none -> 278 us  [the longest x1 205 us: backward_call(): pl.pallas_call(functools.partial(backward_kernel, rows), out_shape=[S((ro...]
    dot_general x40 -> x0, matrix products: 206 us -> none  [the longest x14 99.8 us: times_transposed(): lax.dot_general(first_operand, second_operand, (((1,), (1,)), ((), ())),...]
    ppermute x2 -> x0, waiting for transfers between devices: 138 us -> none  [passed_along(): return lax.ppermute(array, axis, pairs)]
    reshape x6 -> x2, local copies, waits for them, and re-layouts: 28.6 us -> 1.35 us  [the longest x1 0.67 us: unpacked_gains(): kept[:, GAIN_LANES:GAIN_LANES + width].reshape(1, -1)]
    convert_element_type x11 -> x0, local copies, waits for them, and re-layouts: 26.8 us -> none  [the longest x2 7.64 us: backward_unit(): query_grad = query_grad.astype(jnp.bfloat16)]
    convert_element_type x9 -> x1, other arithmetic: 22.6 us -> 0.01 us  [padded_tables(): (jnp.arange(starts.shape[1], dtype=jnp.int32)[None] - starts).astype(jnp....]
    another operation x6 -> x0, other arithmetic: 16.3 us -> none
    unnamed x130 -> x31, local copies, waits for them, and re-layouts: 25.9 us -> 10.2 us
  transfers between devices with their start and end apart: 2 -> 0, of which waited for: 2 -> 0; matrix products, arithmetic and copies ran while one was open for 0% -> 0% of each run, Pallas kernels for 0% -> 0%
where the time goes in v2:
time: 822 us; the launch traced here: 821 us
  Pallas kernels  800 us (97%)
  local copies, waits for them, and re-layouts  14.5 us (2%)
    pallas_call x1, Pallas kernels, scattered(): pl.pallas_call(functools.partial(scatter_kernel, chips, count), out_shape...  267 us
    pallas_call x1, Pallas kernels, gathered(): pl.pallas_call(functools.partial(gather_kernel, chips, count), out_shape=...  256 us
    pallas_call x1, Pallas kernels, backward_call(): pl.pallas_call(functools.partial(backward_kernel, rows), out_shape=[S((ro...  205 us
    pallas_call x1, Pallas kernels, forward_call(): pl.pallas_call(functools.partial(forward_kernel, rows), out_shape=[S((row...  72.2 us

profile of v2, /device:TPU:1, one launch (start us, length us, event | category | flops | bytes accessed | tf_op | source)
XLA Modules:
  0.0 821.0 jit_solution(11199086376641524444)
XLA Ops:
  0.7 0.9 reduce_window_sum.11
  1.5 0.1 select_reduce_fusion.refs_2_
  1.6 0.0 copy-start.9
  1.7 1.3 fusion.6.refs_7_
  2.9 0.8 copy.30
  3.8 1.6 fusion
  5.4 255.6 %gather_weights.1 = (bf16[1536,1536]{1,0:T(8,128)(2,1)}, bf16[1536,768]{1,0:T(8,128)(2,1)}, bf16[1536,768]{1,0:T(8,128)(2,1)}, bf16[1536,1536]{1,0:T(8,128)(2,1)...) custom-call(bf16[96,1536]{1,0:T(8,128)(2,1)} %bitcast.43, ...), custom_call_target="tpu_custom_call" | custom-call | tf_op jit(solution)/shard_map/gather_weights/pallas_call | solution.py:150
  261.0 0.9 slice.20
  261.9 0.7 reshape.78.refs_7_.refs_5_
  262.5 0.7 reshape.77.refs_6_.refs_4_
  263.2 0.0 copy-done.9
  263.2 72.2 %forward_layers.1 = (bf16[384,1536]{1,0:T(8,128)(2,1)}, bf16[384,1536]{1,0:T(8,128)(2,1)}, bf16[384,1536]{1,0:T(8,128)(2,1)}, bf16[384,2048]{1,0:T(8,128)(2,1)},...) custom-call(bf16[384,1536]{1,0:T(8,128)(2,1)} %refs_0_.2, ...), custom_call_target="tpu_custom_call" | custom-call | tf_op jit(solution)/shard_map/forward_layers/pallas_call | solution.py:663
  335.4 205.3 %backward_layers.1 = (bf16[384,1536]{1,0:T(8,128)(2,1)}, f32[8,1536]{1,0:T(8,128)}, f32[8,1536]{1,0:T(8,128)}, bf16[1536,1536]{1,0:T(8,128)(2,1)}, bf16[1536,768...) custom-call(bf16[384,1536]{1,0:T(8,128)(2,1)} %refs_0_.3, ...), custom_call_target="tpu_custom_call" | custom-call | tf_op jit(solution)/shard_map/backward_layers/pallas_call | solution.py:960
  540.7 0.8 reduce_sum.18
  541.6 0.8 reduce_sum.19
  542.4 0.1 reshape.80
  542.5 0.1 reshape.79
  542.6 0.7 pad_bitcast_fusion.refs_7_
  543.2 0.0 copy-start.3
  543.2 267.1 %scatter_grads.1 = (f32[96,1536]{1,0:T(8,128)}, f32[96,768]{1,0:T(8,128)}, f32[96,768]{1,0:T(8,128)}, f32[96,1536]{1,0:T(8,128)}, f32[96,4096]{1,0:T(8,128)}, /*...) custom-call(bf16[1536,1536]{1,0:T(8,128)(2,1)} %get-tuple-element.72, ...), custom_call_target="tpu_custom_call" | custom-call | tf_op jit(solution)/shard_map/scatter_grads/pallas_call | solution.py:317
  810.3 0.0 copy-start.4
  810.4 1.3 fusion.12
  811.7 0.0 copy-done.3
  811.7 0.0 copy-start.6
  811.7 0.0 copy-start.8
  811.7 1.0 copy.45
  812.7 0.0 copy-done.4
  812.7 0.0 copy-start.7
  812.7 0.0 copy-start.5
  812.7 0.0 copy-start.2
  812.7 1.0 copy.46
  813.7 0.0 copy-done.6
  813.7 0.8 copy.47
  814.5 0.0 copy-done.8
  814.5 0.7 copy.48
  815.2 0.0 copy-done.7
  815.2 0.0 copy-start.1
  815.2 0.7 copy.49
  816.0 0.0 copy-done.5
  816.0 0.8 copy.50
  816.8 0.0 copy-done.2
  816.8 1.1 copy.51
  817.9 0.0 copy-done.1
  817.9 0.0 copy-start
  817.9 1.1 copy.52
  819.1 0.8 copy-done
  819.9 1.1 copy.53
  (9 shorter events, 0.1 us)
Async XLA Ops:
  1.6 261.6 %copy-start.9 = (s32[3,128]{1,0:T(4,128)}, s32[3,128]{1,0:T(4,128)S(1)}, u32[]{:S(2)}) copy-start(s32[3,128]{1,0:T(4,128)S(1)} %select_reduce_fusion.refs_2_) | copy-start | bytes 4612
  543.2 268.4 %copy-start.3 = (bf16[384,1536]{1,0:T(8,128)(2,1)S(1)}, bf16[384,1536]{1,0:T(8,128)(2,1)}, u32[]{:S(2)}) copy-start(bf16[384,1536]{1,0:T(8,128)(2,1)} %get-tuple-element.58) | copy-start | bytes 3538948
  810.3 2.3 copy-start.4
  811.7 2.1 copy-start.6
  811.7 2.9 copy-start.8
  812.7 2.6 copy-start.7
  812.7 3.3 copy-start.5
  812.7 4.1 copy-start.2
  815.2 2.7 copy-start.1
  817.9 2.0 copy-start

commit v3 on v2

--- a/solution.py
+++ b/solution.py
@@ -166,181 +166,6 @@
     )(*shards)
 
 
-def scatter_kernel(chips, count, *refs):
-    grads = refs[:count]
-    sums = refs[count : 2 * count]
-    lands = refs[2 * count : 3 * count]
-    rest = refs[3 * count :]
-    firsts = rest[:count]
-    arrivals = rest[count : 2 * count]
-    owns = rest[2 * count : 3 * count]
-    mates = rest[3 * count : 4 * count]
-    ring_send, ring_recv, pair_send, pair_recv, own_load, mate_load = rest[4 * count :]
-    me = lax.axis_index("dp")
-    place, core = ring_place(me, chips)
-    right = ring_device((place + 1) % chips, core, chips)
-    left = ring_device((place + chips - 1) % chips, core, chips)
-    partner = me + 1 - 2 * core
-    barrier = pltpu.get_barrier_semaphore()
-    for other in (right, left, partner):
-        pl.semaphore_signal(barrier, inc=1, device_id={"dp": other}, device_id_type=MESH)
-    pl.semaphore_wait(barrier, 3)
-
-    def owner_chip(way, step):
-        return (place + 2 * chips - 1 - step) % chips if way == 0 else (place + 1 + step) % chips
-
-    def pair_copy(index, way, step):
-        _, _, rows, columns = arrivals[index].shape
-        source = ring_device(owner_chip(way, step), 1 - core, chips)
-        return pltpu.make_async_remote_copy(
-            src_ref=grads[index].at[
-                pl.ds(pl.multiple_of(source * rows, 8), rows), pl.ds(way * columns, columns)
-            ],
-            dst_ref=lands[index].at[way, step],
-            send_sem=pair_send.at[index, way, step],
-            recv_sem=pair_recv.at[index, way, step],
-            device_id={"dp": partner},
-            device_id_type=MESH,
-        )
-
-    def own_copy(index, way, step):
-        _, _, rows, columns = arrivals[index].shape
-        mine = ring_device(owner_chip(way, step), core, chips)
-        return pltpu.make_async_copy(
-            grads[index].at[
-                pl.ds(pl.multiple_of(mine * rows, 8), rows), pl.ds(way * columns, columns)
-            ],
-            owns[index].at[step % 2, way],
-            own_load.at[index, way, step % 2],
-        )
-
-    def mate_copy(index, way, step):
-        return pltpu.make_async_copy(
-            lands[index].at[way, step], mates[index].at[step % 2, way], mate_load.at[index, way, step % 2]
-        )
-
-    def ring_copy(index, way, step, source):
-        return pltpu.make_async_remote_copy(
-            src_ref=source,
-            dst_ref=arrivals[index].at[way, step],
-            send_sem=ring_send.at[index, way, step],
-            recv_sem=ring_recv.at[index, way, step],
-            device_id={"dp": (right, left)[way]},
-            device_id_type=MESH,
-        )
-
-    def start_pair(step, carry):
-        for index in range(count):
-            for way in range(2):
-                pair_copy(index, way, step).start()
-        return carry
-
-    lax.fori_loop(0, chips, start_pair, 0)
-
-    def fetch(step):
-        for index in range(count):
-            for way in range(2):
-                own_copy(index, way, step).start()
-                pair_copy(index, way, step).wait_recv()
-                mate_copy(index, way, step).start()
-
-    def added(index, way, step, extra, target, kind):
-        _, _, rows, columns = arrivals[index].shape
-        own_copy(index, way, step).wait()
-        mate_copy(index, way, step).wait()
-        part = 32 if rows % 32 == 0 else 8
-        slot = step % 2
-
-        def piece(at, carry):
-            band = pl.ds(pl.multiple_of(at * part, part), part)
-            value = owns[index][slot, way, band, :].astype(jnp.float32) + mates[index][
-                slot, way, band, :
-            ].astype(jnp.float32)
-            if extra is not None:
-                value = value + extra[band, :].astype(jnp.float32)
-            target[band, :] = value.astype(kind)
-            return carry
-
-        lax.fori_loop(0, rows // part, piece, 0)
-
-    fetch(0)
-    fetch(1)
-    for index in range(count):
-        for way in range(2):
-            added(index, way, 0, None, firsts[index].at[way], firsts[index].dtype)
-        for way in range(2):
-            ring_copy(index, way, 0, firsts[index].at[way]).start()
-
-    def hop(step, carry):
-        fetch(step + 1)
-        for index in range(count):
-            for way in range(2):
-                here = arrivals[index].at[way, step - 1]
-                ring_copy(index, way, step - 1, here).wait_recv()
-                added(index, way, step, here, here, here.dtype)
-            for way in range(2):
-                ring_copy(index, way, step, arrivals[index].at[way, step - 1]).start()
-        return carry
-
-    lax.fori_loop(1, chips - 1, hop, 0)
-    for index in range(count):
-        _, _, rows, columns = arrivals[index].shape
-        for way in range(2):
-            here = arrivals[index].at[way, chips - 2]
-            ring_copy(index, way, chips - 2, here).wait_recv()
-            added(
-                index, way, chips - 1, here, sums[index].at[:, pl.ds(way * columns, columns)], jnp.float32
-            )
-
-    def finish(step, carry):
-        for index in range(count):
-            for way in range(2):
-                ring_copy(index, way, step, firsts[index].at[way]).wait_send()
-        return carry
-
-    lax.fori_loop(0, chips - 1, finish, 0)
-
-    def finish_pair(step, carry):
-        for index in range(count):
-            for way in range(2):
-                pair_copy(index, way, step).wait_send()
-        return carry
-
-    lax.fori_loop(0, chips, finish_pair, 0)
-
-
-def scattered(grads, chips):
-    count = len(grads)
-    steps = chips - 1
-    half = [(g.shape[0] // (2 * chips), g.shape[1] // 2) for g in grads]
-    kinds = [g.dtype for g in grads]
-    outs = pl.pallas_call(
-        functools.partial(scatter_kernel, chips, count),
-        out_shape=[jax.ShapeDtypeStruct((r, 2 * c), jnp.float32) for r, c in half]
-        + [jax.ShapeDtypeStruct((2, chips, r, c), k) for (r, c), k in zip(half, kinds)],
-        in_specs=[pl.BlockSpec(memory_space=pl.ANY)] * count,
-        out_specs=[pl.BlockSpec(memory_space=pltpu.VMEM)] * count
-        + [pl.BlockSpec(memory_space=pl.ANY)] * count,
-        scratch_shapes=[pltpu.VMEM((2, r, c), k) for (r, c), k in zip(half, kinds)]
-        + [pltpu.VMEM((2, steps, r, c), k) for (r, c), k in zip(half, kinds)]
-        + [pltpu.VMEM((2, 2, r, c), k) for (r, c), k in zip(half, kinds)]
-        + [pltpu.VMEM((2, 2, r, c), k) for (r, c), k in zip(half, kinds)]
-        + [
-            pltpu.SemaphoreType.DMA((count, 2, steps)),
-            pltpu.SemaphoreType.DMA((count, 2, steps)),
-            pltpu.SemaphoreType.DMA((count, 2, chips)),
-            pltpu.SemaphoreType.DMA((count, 2, chips)),
-            pltpu.SemaphoreType.DMA((count, 2, 2)),
-            pltpu.SemaphoreType.DMA((count, 2, 2)),
-        ],
-        compiler_params=pltpu.CompilerParams(
-            collective_id=1, has_side_effects=True, vmem_limit_bytes=60 << 20
-        ),
-        name="scatter_grads",
-    )(*grads)
-    return outs[:count]
-
-
 HEADS = 16
 KV_HEADS = 8
 HD = 96
@@ -348,6 +173,7 @@
 ROPE_BASE = 100000.0
 SCALE = 1.0 / math.sqrt(HD)
 GAIN_LANES = 128
+VMEM_MOST = 67_043_328
 
 
 def row_starts(lengths, row_length):
@@ -366,15 +192,6 @@
 def unpacked_gains(whole, width):
     kept = whole.reshape(-1, 16, 2 * GAIN_LANES)[:, 0].astype(jnp.float32)
     return kept[:, :width].reshape(1, -1), kept[:, GAIN_LANES : GAIN_LANES + width].reshape(1, -1)
-
-
-def packed_gain_sums(first, second, width):
-    edge = ((0, 0), (0, GAIN_LANES - width))
-    joined = jnp.concatenate(
-        [jnp.pad(first.reshape(-1, width), edge), jnp.pad(second.reshape(-1, width), edge)], axis=1
-    )
-    spread = jnp.pad(joined[:, None, :], ((0, 0), (0, 7), (0, 0)))
-    return spread.reshape(-1, 2 * GAIN_LANES)
 
 
 def spread_heads(tile, lane):
@@ -728,23 +545,192 @@
     lax.fori_loop(0, rows // band_rows, body, 0)
 
 
-def backward_kernel(rows, *refs):
+class Unit:
+    def __init__(self, index, piece, total, rows, columns, stage, first_column):
+        self.index, self.piece, self.total, self.rows, self.columns = index, piece, total, rows, columns
+        self.stage, self.first_column = stage, first_column
+
+
+def backward_kernel(rows, chips, *refs):
     (cotangent, cosine, fore, aft, gain_one, gain_two,
      w_query, w_key, w_value, w_out, w_gate, w_up, w_down,
-     source_i, attn_input_i, queries_i, keys_i, values_i, probs_i, attended_i, mid_i, ffn_input_i, gate_i, up_i, activated_i,
-     out_ref, gain_one_o, gain_two_o, g_query, g_key, g_value, g_out, g_gate, g_up, g_down,
-     incoming, passed, activated, ffn_input, attn_input, attended, source, mid, probs, queries, keys, values,
+     source_i, attn_input_i, queries_i, keys_i, values_i, probs_i, attended_i, mid_i, ffn_input_i, gate_i, up_i, activated_i) = refs[:25]
+    refs = refs[25:]
+    out_ref, s_query, s_key, s_value, s_out, s_gate, s_up, s_down, s_gain = refs[:9]
+    g_query, g_key, g_value, g_out, g_gate, g_up, g_down = refs[9:16]
+    lands, arrivals = refs[16:27], refs[27:38]
+    (incoming, passed, ffn_input, attn_input, attended, source, mid, probs, queries, keys, values,
      gate_grad, up_grad, stream_grad, out_grad, heads_grad, query_grad, key_grad, value_grad,
-     gate_slot, flat, kv_slot, pair_slot, flat_stage, wide_stage,
-     gate_sem, flat_sem, kv_sem, pair_sem, flat_out, wide_out, load_sem, send_sem, recv_sem) = refs
+     gate_slot, flat, kv_slot, pair_slot, flat_stage,
+     gate_sem, flat_sem, kv_sem, pair_sem, flat_out, wide_out, load_sem, send_sem, recv_sem,
+     gain_sum_one, gain_sum_two, gain_pack,
+     own_a, mate_a, sum_a, full_a, own_b, mate_b, sum_b, full_b, own_c, mate_c, sum_c, full_c,
+     ring_send, ring_recv, mate_send, mate_recv, own_sem, mate_sem, sum_sem, full_sem) = refs[38:]
     section = lax.axis_index("pipe")
     width = cotangent.shape[1]
     inner = w_gate.shape[1]
     kv_width = w_key.shape[1]
     micro = rows // MB
+    me = lax.axis_index("dp")
+    place, core = ring_place(me, chips)
+    right = ring_device((place + 1) % chips, core, chips)
+    left = ring_device((place + chips - 1) % chips, core, chips)
+    partner = me + 1 - 2 * core
     barrier = pltpu.get_barrier_semaphore()
+    for other in (right, left, partner):
+        pl.semaphore_signal(barrier, inc=1, device_id={"dp": other}, device_id_type=MESH)
     pl.semaphore_signal(barrier, inc=1, device_id={"pipe": 1 - section}, device_id_type=MESH)
-    pl.semaphore_wait(barrier, 1)
+    pl.semaphore_wait(barrier, 4)
+
+    def in_rows(grad, shard_rows, columns, first_column):
+        half = grad.shape[1] // 2
+
+        def piece(device, way):
+            return grad.at[
+                pl.ds(pl.multiple_of(device * shard_rows, 8), shard_rows),
+                pl.ds(way * half + first_column, columns),
+            ]
+
+        return piece
+
+    units = []
+
+    def unit(grad, total, stage, split):
+        shard_rows = total.shape[0]
+        columns = total.shape[1] // 2 // split
+        for at in range(split):
+            piece = in_rows(grad, shard_rows, columns, at * columns)
+            units.append(Unit(len(units), piece, total, shard_rows, columns, stage[at], at * columns))
+
+    bank_a = [(own_a.at[i], mate_a.at[i], sum_a.at[i], full_a) for i in range(2)]
+    bank_b = [(own_b.at[i], mate_b.at[i], sum_b.at[i], full_b) for i in range(4)]
+    unit(g_down, s_down, bank_a, 2)
+    unit(g_gate, s_gate, bank_b[:2], 2)
+    unit(g_up, s_up, bank_b[2:], 2)
+    unit(g_out, s_out, bank_b[:1], 1)
+    unit(g_query, s_query, bank_b[1:2], 1)
+    unit(g_key, s_key, bank_b[2:3], 1)
+    unit(g_value, s_value, bank_b[3:4], 1)
+    units.append(
+        Unit(len(units), lambda device, way: gain_pack.at[device, :, pl.ds(way * 128, 128)], s_gain, 8, 128,
+             (own_c, mate_c, sum_c, full_c), 0)
+    )
+
+    def owner_chip(way, step):
+        return (place + 2 * chips - 1 - step) % chips if way == 0 else (place + 1 + step) % chips
+
+    def mate_exchange(u, way, step):
+        return pltpu.make_async_remote_copy(
+            src_ref=u.piece(ring_device(owner_chip(way, step), 1 - core, chips), way),
+            dst_ref=lands[u.index].at[way, step],
+            send_sem=mate_send.at[u.index, way, step], recv_sem=mate_recv.at[u.index, way, step],
+            device_id={"dp": partner}, device_id_type=MESH,
+        )
+
+    def own_load(u, way, step):
+        return pltpu.make_async_copy(
+            u.piece(ring_device(owner_chip(way, step), core, chips), way),
+            u.stage[0].at[way, :, pl.ds(0, u.columns)], own_sem.at[u.index, way],
+        )
+
+    def mate_load(u, way, step):
+        return pltpu.make_async_copy(
+            lands[u.index].at[way, step], u.stage[1].at[way, :, pl.ds(0, u.columns)], mate_sem.at[u.index, way]
+        )
+
+    def running(u, way, step):
+        return u.stage[2].at[step % 2, way, :, pl.ds(0, u.columns)]
+
+    def sum_load(u, way, step):
+        return pltpu.make_async_copy(
+            arrivals[u.index].at[way, step - 1], running(u, way, step), sum_sem.at[u.index, way]
+        )
+
+    def ring_copy(u, way, step):
+        return pltpu.make_async_remote_copy(
+            src_ref=running(u, way, step), dst_ref=arrivals[u.index].at[way, step],
+            send_sem=ring_send.at[u.index, way, step], recv_sem=ring_recv.at[u.index, way, step],
+            device_id={"dp": (right, left)[way]}, device_id_type=MESH,
+        )
+
+    def start_exchange(group):
+        def body(step, carry):
+            for u in group:
+                for way in range(2):
+                    mate_exchange(u, way, step).start()
+            return carry
+
+        lax.fori_loop(0, chips, body, 0)
+        for u in group:
+            load_terms(u, 0)
+
+    def load_terms(u, step):
+        for way in range(2):
+            own_load(u, way, step).start()
+            mate_exchange(u, way, step).wait_recv()
+            mate_load(u, way, step).start()
+
+    def visit(u, step, first=False, last=False):
+        if not first:
+            for way in range(2):
+                ring_copy(u, way, step - 1).wait_recv()
+                if isinstance(step, int):
+                    if step >= 2:
+                        ring_copy(u, way, step - 2).wait_send()
+                else:
+
+                    @pl.when(step >= 2)
+                    def _():
+                        ring_copy(u, way, step - 2).wait_send()
+
+                sum_load(u, way, step).start()
+        part = 32 if u.rows % 32 == 0 else 8
+        for way in range(2):
+            own_load(u, way, step).wait()
+            mate_load(u, way, step).wait()
+            if not first:
+                sum_load(u, way, step).wait()
+            here = running(u, way, step)
+            columns = pl.ds(0, u.columns)
+
+            def add(at, carry):
+                band = pl.ds(pl.multiple_of(at * part, part), part)
+                value = u.stage[0][way, band, columns].astype(jnp.float32)
+                value = value + u.stage[1][way, band, columns].astype(jnp.float32)
+                if not first:
+                    value = value + here[band, :].astype(jnp.float32)
+                if last:
+                    u.stage[3][way, band, columns] = value
+                else:
+                    here[band, :] = value.astype(here.dtype)
+                return carry
+
+            lax.fori_loop(0, u.rows // part, add, 0)
+        if last:
+            puts = []
+            for way in range(2):
+                column = way * (u.total.shape[1] // 2) + u.first_column
+                puts.append(
+                    pltpu.make_async_copy(
+                        u.stage[3].at[way, :, pl.ds(0, u.columns)], u.total.at[:, pl.ds(column, u.columns)], full_sem.at[way]
+                    )
+                )
+                puts[-1].start()
+            for put in puts:
+                put.wait()
+            for way in range(2):
+                ring_copy(u, way, step - 1).wait_send()
+        else:
+            load_terms(u, step + 1)
+            for way in range(2):
+                ring_copy(u, way, step).start()
+
+    def visits(group, step, first=False, last=False):
+        for u in group:
+            visit(u, step, first, last)
+
+    down_units, gate_units, up_units, square_units, small_units = units[:2], units[2:4], units[4:6], units[6:8], units[8:]
+    hops = chips - 1
 
     def pass_on(part):
         band = pl.ds(part * MB, MB)
@@ -759,7 +745,6 @@
         copy.start()
         return copy
 
-    act_load = loading(0, activated_i, activated)
     mid_load = loading(1, mid_i, mid)
     rest_loads = [
         loading(2 + i, there, here)
@@ -816,29 +801,97 @@
         for part in range(micro):
             pass_on(part).wait_recv()
 
-    def staged(left, left_step, right, stage, sems, targets):
-        count = left.shape[1] // left_step
-        columns = right.shape[1]
-
-        def put(j, slot):
-            band = pl.ds(pl.multiple_of(j * left_step, left_step), left_step)
-            return pltpu.make_async_copy(
-                stage.at[slot, :, pl.ds(0, columns)], targets.at[band, :], sems.at[slot]
-            )
+    def put_tile(stage, sems, target, j, size, columns):
+        band = pl.ds(pl.multiple_of(j * size, size), size)
+        return pltpu.make_async_copy(
+            stage.at[j % 2, :, pl.ds(0, columns)], target.at[band, :], sems.at[j % 2]
+        )
+
+    def product_tile(left_ref, right_ref, stage, sems, target, j, size):
+        columns = right_ref.shape[1]
+
+        @pl.when(j >= 2)
+        def _():
+            put_tile(stage, sems, target, j - 2, size, columns).wait()
+
+        column = pl.ds(pl.multiple_of(j * size, size), size)
+        stage[j % 2, :, pl.ds(0, columns)] = dot_tn(left_ref[:, column], right_ref[...]).astype(jnp.bfloat16)
+        put_tile(stage, sems, target, j, size, columns).start()
+
+    def product_end(count, right_ref, stage, sems, target, size):
+        for j in range(max(0, count - 2), count):
+            put_tile(stage, sems, target, j, size, right_ref.shape[1]).wait()
+
+    def product(left_ref, right_ref, stage, sems, target, size):
+        count = left_ref.shape[1] // size
 
         def body(j, carry):
+            product_tile(left_ref, right_ref, stage, sems, target, j, size)
+            return carry
+
+        lax.fori_loop(0, count, body, 0)
+        product_end(count, right_ref, stage, sems, target, size)
+
+    def tile_load(j):
+        column = pl.ds(pl.multiple_of(j * step, step), step)
+        return pltpu.make_async_copy(
+            activated_i.at[:, column], gate_slot.at[2, j % 2], gate_sem.at[2, j % 2]
+        )
+
+    def down_start():
+        count = inner // step
+        tile_load(0).start()
+
+        def body(j, carry):
+            @pl.when(j + 1 < count)
+            def _():
+                tile_load(j + 1).start()
+
             @pl.when(j >= 2)
             def _():
-                put(j - 2, j % 2).wait()
-
-            column = pl.ds(pl.multiple_of(j * left_step, left_step), left_step)
-            stage[j % 2, :, pl.ds(0, columns)] = dot_tn(left[:, column], right[...]).astype(jnp.bfloat16)
-            put(j, j % 2).start()
+                put_tile(flat_stage, flat_out, g_down, j - 2, step, width).wait()
+
+            tile_load(j).wait()
+            flat_stage[j % 2] = dot_tn(gate_slot[2, j % 2], incoming[...]).astype(jnp.bfloat16)
+            put_tile(flat_stage, flat_out, g_down, j, step, width).start()
             return carry
 
         lax.fori_loop(0, count, body, 0)
-        for j in range(max(0, count - 2), count):
-            put(j, j % 2).wait()
+        product_end(count, incoming, flat_stage, flat_out, g_down, step)
+        start_exchange(down_units)
+        visits(down_units, 0, first=True)
+
+
+    def pack_gains():
+        shard_width = width // (2 * chips)
+        for way, sums in enumerate((gain_sum_one, gain_sum_two)):
+            for device in range(2 * chips):
+                offset = device * shard_width
+                base = offset // 128 * 128
+                if base + 128 < width:
+                    span = sums[:, base : base + 256]
+                    span = pltpu.roll(span, (256 - (offset - base)) % 256, 1)
+                else:
+                    span = sums[:, base : base + 128]
+                    span = pltpu.roll(span, (128 - (offset - base)) % 128, 1)
+                gain_pack[device, :, pl.ds(way * 128, 128)] = span[:, :128]
+
+    def down_early(at, carry):
+        visits(down_units, at)
+        return carry
+
+    early = min(5, hops - 1)
+
+    def early_hop(at):
+        if at <= early:
+
+            @pl.when(section == 0)
+            def _():
+                visits(down_units, at)
+
+    @pl.when(section == 0)
+    def _():
+        down_start()
 
     def contract_back(j, slot):
         column = pl.ds(pl.multiple_of(j * step, step), step)
@@ -850,6 +903,7 @@
         up_grad[:, column] = (act_grad * gate * sigmoid).astype(jnp.bfloat16)
 
     streamed(inner // step, 3, down_copies, contract_back)
+    early_hop(1)
     lead(width // step, 3, out_copies)
 
     def expand_back(j, slot):
@@ -857,8 +911,9 @@
         stream_grad[:, column] = dot_nt(gate_grad[...], pair_slot[slot, 0]) + dot_nt(up_grad[...], pair_slot[slot, 1])
 
     streamed(width // short, 2, ffn_copies, expand_back)
+    early_hop(2)
     mid_load.wait()
-    norm_back(stream_grad, mid, gain_two, incoming, mid, out_grad, gain_two_o, rows)
+    norm_back(stream_grad, mid, gain_two, incoming, mid, out_grad, gain_sum_two, rows)
     lane = lax.broadcasted_iota(jnp.int32, (rows, 128), 1)
 
     def attended_back(j, slot):
@@ -866,13 +921,14 @@
         stream_grad[:, column] = dot_nt(out_grad[...], flat[slot])
 
     streamed(width // step, 3, out_copies, attended_back)
-    lead(width // step, 3, qkv_copies)
+    lead(width // step, 2, qkv_copies)
     for part in range(width // 384):
         tile = stream_grad[:, pl.ds(part * 384, 384)]
         for k, head in enumerate(spread_heads(tile, lane)):
             heads_grad[:, pl.ds((part * 4 + k) * 128, 128)] = jnp.where(lane < HD, head, 0.0).astype(jnp.bfloat16)
     for copy in rest_loads:
         copy.wait()
+    early_hop(3)
 
     def attend_back(at, carry):
         row = at // 2
@@ -912,6 +968,7 @@
         return carry
 
     lax.fori_loop(0, 2 * micro, attend_back, 0)
+    early_hop(4)
 
     def project_back(j, slot):
         column = pl.ds(pl.multiple_of(j * step, step), step)
@@ -921,8 +978,8 @@
             + dot_nt(value_grad[...], kv_slot[slot, 1])
         )
 
-    streamed(width // step, 3, qkv_copies, project_back)
-    norm_back(stream_grad, source, gain_one, mid, None, passed, gain_one_o, rows)
+    streamed(width // step, 2, qkv_copies, project_back)
+    norm_back(stream_grad, source, gain_one, mid, None, passed, gain_sum_one, rows)
 
     @pl.when(section == 1)
     def _():
@@ -930,15 +987,90 @@
             pass_on(part).start()
 
     keep = loading(11, passed, out_ref)
-    act_load.wait()
-    staged(activated, step, incoming, flat_stage, flat_out, g_down)
-    staged(ffn_input, short, gate_grad, wide_stage, wide_out, g_gate)
-    staged(ffn_input, short, up_grad, wide_stage, wide_out, g_up)
-    staged(attended, step, out_grad, flat_stage, flat_out, g_out)
-    staged(attn_input, step, query_grad, flat_stage, flat_out, g_query)
-    staged(attn_input, step, key_grad, flat_stage, flat_out, g_key)
-    staged(attn_input, step, value_grad, flat_stage, flat_out, g_value)
+    early_hop(5)
+
+    @pl.when(section == 1)
+    def _():
+        down_start()
+        lax.fori_loop(1, early + 1, down_early, 0)
+    pack_gains()
+    wide_stage = pair_slot.at[0]
+    product(ffn_input, gate_grad, wide_stage, wide_out, g_gate, short)
+    start_exchange(gate_units)
+
+    def down_hop(at, carry):
+        visits(down_units, at)
+        return carry
+
+    lax.fori_loop(early + 1, hops, down_hop, 0)
+    visits(gate_units, 0, first=True)
+    visits(down_units, hops, last=True)
+    wide_count = width // short
+
+    def gate_hop(at, carry):
+        visits(gate_units, at)
+
+        @pl.when(at <= wide_count)
+        def _():
+            product_tile(ffn_input, up_grad, wide_stage, wide_out, g_up, at - 1, short)
+
+        return carry
+
+    lax.fori_loop(1, hops, gate_hop, 0)
+    product_end(wide_count, up_grad, wide_stage, wide_out, g_up, short)
+    start_exchange(up_units)
+    visits(up_units, 0, first=True)
+    visits(gate_units, hops, last=True)
+    flat_count = width // step
+
+    def up_hop(at, carry):
+        visits(up_units, at)
+
+        @pl.when(at <= flat_count)
+        def _():
+            product_tile(attended, out_grad, flat_stage, flat_out, g_out, at - 1, step)
+
+        return carry
+
+    lax.fori_loop(1, flat_count + 1, up_hop, 0)
+    product_end(flat_count, out_grad, flat_stage, flat_out, g_out, step)
+
+    def up_hop_more(at, carry):
+        visits(up_units, at)
+
+        @pl.when(at <= 2 * flat_count)
+        def _():
+            product_tile(attn_input, query_grad, flat_stage, flat_out, g_query, at - 1 - flat_count, step)
+
+        return carry
+
+    lax.fori_loop(flat_count + 1, hops, up_hop_more, 0)
+    product_end(flat_count, query_grad, flat_stage, flat_out, g_query, step)
+    start_exchange(square_units)
+    visits(square_units, 0, first=True)
+    product(attn_input, key_grad, flat_stage, flat_out, g_key, step)
+    product(attn_input, value_grad, flat_stage, flat_out, g_value, step)
+    visits(up_units, hops, last=True)
+    start_exchange(small_units)
+    visits(small_units, 0, first=True)
+
+    def last_hop(at, carry):
+        visits(square_units, at)
+        visits(small_units, at)
+        return carry
+
+    lax.fori_loop(1, hops, last_hop, 0)
+    visits(square_units, hops, last=True)
+    visits(small_units, hops, last=True)
     keep.wait()
+
+    def settle(at, carry):
+        for u in units:
+            for way in range(2):
+                mate_exchange(u, way, at).wait_send()
+        return carry
+
+    lax.fori_loop(0, chips, settle, 0)
 
     @pl.when(section == 1)
     def _():
@@ -946,7 +1078,7 @@
             pass_on(part).wait_send()
 
 
-def backward_call(cotangent, tables, gain_one, gain_two, weights, source, kept):
+def backward_call(cotangent, tables, gain_one, gain_two, weights, source, kept, chips):
     rows, width = cotangent.shape
     micro = rows // MB
     inner = weights[4].shape[1]
@@ -957,26 +1089,39 @@
     local = pl.BlockSpec(memory_space=pltpu.VMEM)
     V = pltpu.VMEM
     D = pltpu.SemaphoreType.DMA
+    shards_n = 2 * chips
+    sums = [S((w.shape[0] // shards_n, w.shape[1]), full) for w in weights] + [S((8, 256), full)]
+    pieces = [(inner // shards_n, width // 4, low)] * 2 + [(width // shards_n, inner // 4, low)] * 4
+    pieces += [(width // shards_n, width // 2, low)] * 2 + [(width // shards_n, kv_width // 2, low)] * 2 + [(8, 128, full)]
+    count = len(pieces)
+    tall, slim = inner // shards_n, width // shards_n
+    quarter, wide = width // 4, inner // 4
     outs = pl.pallas_call(
-        functools.partial(backward_kernel, rows),
-        out_shape=[S((rows, width), low), S((8, width), full), S((8, width), full)]
-        + [S(w.shape, low) for w in weights],
+        functools.partial(backward_kernel, rows, chips),
+        out_shape=[S((rows, width), low)] + sums + [S(w.shape, low) for w in weights]
+        + [S((2, chips, r, c), k) for r, c, k in pieces] + [S((2, chips - 1, r, c), k) for r, c, k in pieces],
         in_specs=[anywhere] + [local] * 5 + [anywhere] * (8 + len(kept)),
-        out_specs=[anywhere, local, local] + [anywhere] * 7,
+        out_specs=[anywhere] * (1 + len(sums) + 7 + 2 * count),
         scratch_shapes=[
             V((rows, width), low), V((rows, width), low),
-            V((rows, inner), low), V((rows, width), low), V((rows, width), low), V((rows, width), low), V((rows, width), low),
+            V((rows, width), low), V((rows, width), low), V((rows, width), low), V((rows, width), low),
             V((rows, width), full), V(kept[4].shape, low), V(kept[1].shape, low), V(kept[2].shape, low), V(kept[3].shape, low),
             V((rows, inner), low), V((rows, inner), low), V((rows, width), full), V((rows, width), low), V((rows, HEADS * 128), low),
             V((rows, width), low), V((rows, kv_width), low), V((rows, kv_width), low),
-            V((3, 2, rows, 512), low), V((3, 512, width), low), V((3, 2, 512, kv_width), low), V((2, 2, 256, inner), low),
-            V((2, 512, width), low), V((2, 256, inner), low),
+            V((3, 2, rows, 512), low), V((3, 512, width), low), V((2, 2, 512, kv_width), low), V((2, 2, 256, inner), low),
+            V((2, 512, width), low),
             D((3, 2)), D((3,)), D((3, 2)), D((2, 2)), D((2,)), D((2,)), D((12,)), D((micro,)), D((micro,)),
+            V((8, width), full), V((8, width), full), V((shards_n, 8, 256), full),
+            V((2, 2, tall, quarter), low), V((2, 2, tall, quarter), low), V((2, 2, 2, tall, quarter), low), V((2, tall, quarter), full),
+            V((4, 2, slim, wide), low), V((4, 2, slim, wide), low), V((4, 2, 2, slim, wide), low), V((2, slim, wide), full),
+            V((2, 8, 128), full), V((2, 8, 128), full), V((2, 2, 8, 128), full), V((2, 8, 128), full),
+            D((count, 2, chips - 1)), D((count, 2, chips - 1)), D((count, 2, chips)), D((count, 2, chips)),
+            D((count, 2)), D((count, 2)), D((count, 2)), D((2,)),
         ],
-        compiler_params=pltpu.CompilerParams(collective_id=3, has_side_effects=True, vmem_limit_bytes=63 << 20),
+        compiler_params=pltpu.CompilerParams(collective_id=3, has_side_effects=True, vmem_limit_bytes=VMEM_MOST),
         name="backward_layers",
     )(cotangent, *tables, gain_one, gain_two, *weights, source, *kept)
-    return outs[0], outs[1].sum(axis=0), outs[2].sum(axis=0), list(outs[3:])
+    return outs[0], outs[1 : 1 + len(sums)]
 
 
 def shards(
@@ -991,17 +1136,14 @@
     weights = wholes[:7]
     gain_one, gain_two = unpacked_gains(wholes[7], width)
     result, source, kept = forward_call(tokens, starts, tables, gain_one, gain_two, weights)
-    input_grad, gain_one_grad, gain_two_grad, terms = backward_call(
-        cotangent, tables, gain_one, gain_two, weights, source, kept
-    )
-    sums = scattered(terms + [packed_gain_sums(gain_one_grad, gain_two_grad, width)], chips)
-    gains = sums[7]
+    input_grad, sums = backward_call(cotangent, tables, gain_one, gain_two, weights, source, kept, chips)
+    gains = sums[7].sum(axis=0, keepdims=True)
     return (
         result[None],
         input_grad[None],
         *(item[None] for item in sums[:7]),
-        gains[:1, :width],
-        gains[:1, GAIN_LANES : GAIN_LANES + width],
+        gains[:, :width],
+        gains[:, GAIN_LANES : GAIN_LANES + width],
     )
 
 

time: 822 us -> 773 us (0.940)
  Pallas kernels: 800 us -> 750 us
    pallas_call x2 -> x1, Pallas kernels: 472 us -> 422 us  [backward_call(): pl.pallas_call(functools.partial(backward_kernel, rows, chips), out_shape...]
where the time goes in v3:
time: 773 us; the launch traced here: 770 us
  Pallas kernels  750 us (97%)
  local copies, waits for them, and re-layouts  14.4 us (2%)
    pallas_call x1, Pallas kernels, backward_call(): pl.pallas_call(functools.partial(backward_kernel, rows, chips), out_shape...  422 us
    pallas_call x1, Pallas kernels, gathered(): pl.pallas_call(functools.partial(gather_kernel, chips, count), out_shape=...  256 us
    pallas_call x1, Pallas kernels, forward_call(): pl.pallas_call(functools.partial(forward_kernel, rows), out_shape=[S((row...  72.1 us

profile of v3, /device:TPU:1, one launch (start us, length us, event | category | flops | bytes accessed | tf_op | source)
XLA Modules:
  0.0 769.7 jit_solution(10505402695847036385)
XLA Ops:
  0.7 0.9 reduce_window_sum.11
  1.5 0.1 select_reduce_fusion.refs_2_
  1.6 0.0 copy-start.8
  1.7 1.3 fusion.6.refs_7_
  2.9 0.8 copy.30
  3.8 1.6 fusion
  5.4 255.6 %gather_weights.1 = (bf16[1536,1536]{1,0:T(8,128)(2,1)}, bf16[1536,768]{1,0:T(8,128)(2,1)}, bf16[1536,768]{1,0:T(8,128)(2,1)}, bf16[1536,1536]{1,0:T(8,128)(2,1)...) custom-call(bf16[96,1536]{1,0:T(8,128)(2,1)} %bitcast.42, ...), custom_call_target="tpu_custom_call" | custom-call | tf_op jit(solution)/shard_map/gather_weights/pallas_call | solution.py:150
  261.0 0.9 slice.20
  261.9 0.7 reshape.69.refs_7_.refs_5_
  262.5 0.7 reshape.68.refs_6_.refs_4_
  263.2 0.0 copy-done.8
  263.2 72.1 %forward_layers.1 = (bf16[384,1536]{1,0:T(8,128)(2,1)}, bf16[384,1536]{1,0:T(8,128)(2,1)}, bf16[384,1536]{1,0:T(8,128)(2,1)}, bf16[384,2048]{1,0:T(8,128)(2,1)},...) custom-call(bf16[384,1536]{1,0:T(8,128)(2,1)} %refs_0_.2, ...), custom_call_target="tpu_custom_call" | custom-call | tf_op jit(solution)/shard_map/forward_layers/pallas_call | solution.py:480
  335.4 422.2 %backward_layers.1 = (bf16[384,1536]{1,0:T(8,128)(2,1)}, f32[96,1536]{1,0:T(8,128)}, f32[96,768]{1,0:T(8,128)}, f32[96,768]{1,0:T(8,128)}, f32[96,1536]{1,0:T(8,...) custom-call(bf16[384,1536]{1,0:T(8,128)(2,1)} %refs_0_.3, ...), custom_call_target="tpu_custom_call" | custom-call | tf_op jit(solution)/shard_map/backward_layers/pallas_call | solution.py:1099
  757.6 0.0 copy-start.3
  757.6 0.8 reduce_sum.9
  758.4 0.5 fusion.12
  758.9 0.0 copy-start.5
  758.9 0.0 copy-start.7
  758.9 2.4 copy.45
  761.4 0.0 copy-done.3
  761.4 0.0 copy-start.6
  761.4 0.0 copy-start.4
  761.4 0.0 copy-start.2
  761.4 1.0 copy.46
  762.4 0.0 copy-done.5
  762.4 0.8 copy.47
  763.2 0.0 copy-done.7
  763.2 0.7 copy.48
  763.9 0.0 copy-done.6
  763.9 0.0 copy-start.1
  763.9 0.7 copy.49
  764.6 0.0 copy-done.4
  764.6 0.8 copy.50
  765.5 0.0 copy-done.2
  765.5 1.1 copy.51
  766.6 0.0 copy-done.1
  766.6 0.0 copy-start
  766.6 1.1 copy.52
  767.8 0.8 copy-done
  768.6 1.1 copy.53
  (7 shorter events, 0.0 us)
Async XLA Ops:
  1.6 261.6 %copy-start.8 = (s32[3,128]{1,0:T(4,128)}, s32[3,128]{1,0:T(4,128)S(1)}, u32[]{:S(2)}) copy-start(s32[3,128]{1,0:T(4,128)S(1)} %select_reduce_fusion.refs_2_) | copy-start | bytes 4612
  757.6 3.8 copy-start.3
  758.9 3.5 copy-start.5
  758.9 4.3 copy-start.7
  761.4 2.6 copy-start.6
  761.4 3.3 copy-start.4
  761.4 4.1 copy-start.2
  763.9 2.7 copy-start.1
  766.6 2.0 copy-start
